TPU v7x, 256 devices: a whole 4x4x8 slice. The times are simulated.
256 devices in a mesh: row: 8 (over x, y_hi), col: 32 (over z, y_lo, core).
Axes of the slice: x: 4, y: 4 (y_hi: 2, y_lo: 2; y = y_hi * 2 + y_lo), z: 8, core: 2. Of those that a mesh axis runs over, the one named last changes fastest.
Arguments:
- boxes: int32 [4, 65536], P(None, 'col'), may hold values from 0 to 4095, as said below
- pins: int32 [65536], P('col'), may hold values from 2 to 64
- capacity: float32 [4096, 4096], P('row', 'col'), may hold values from 4 to 12
- cell_bin: int32 [8, 65536], P('row', 'col'), may hold values from 0 to 65535
- cell_area: float32 [8, 65536], P('row', 'col'), may hold values from 1 to 10
Outputs:
- rudy: float32 [4096, 4096], P('row', 'col')
- inflation: float32 [4096, 4096], P('row', 'col')
- cell_sizes: float32 [8, 65536], P('row', 'col')
Inputs may be any that keep to these rules, and one draw needn't show every extreme that they name: `boxes`: row 0 and 1 are a net's first and last bin column, row 2 and 3 its first and last bin row; first <= last, a box spans at most 512 columns and 512 rows.
All inputs are finite; a program needn't handle non-finite values.
Results may differ from a plain program's by a relative error of at most 0.0003.
Values sent between devices are 32-bit elements; how exact they have to be, the bound alone decides.
A program may use at most 64 MiB of HBM per device.

v0:
```python
import functools

import jax
import jax.numpy as jnp
from jax import lax
from jax.sharding import Mesh
from jax.sharding import PartitionSpec as P

ROW = ("row_0", "row_1")
COL = ("col_0", "col_1", "col_2")
ROW_COL = ("row_0", "row_1", "col_0", "col_1", "col_2")


def joined_along(pieces, dim):
    pieces = jnp.moveaxis(pieces, 0, dim)
    dims = pieces.shape
    return pieces.reshape(*dims[:dim], dims[dim] * dims[dim + 1], *dims[dim + 2 :])


def copy_for_each(shard, axis):
    peers = lax.axis_size(axis)
    return lax.all_to_all(
        jnp.broadcast_to(shard[None], (peers, *shard.shape)), axis, 0, 0, tiled=True
    )


def collect(shard, axis, dim):
    return joined_along(copy_for_each(shard, axis), dim)


def one_axis_at_a_time(shard, axes):
    return functools.reduce(lax.psum, axes, shard)


def raster(table, row_start, row_count, col_count):
    total_nets = table.shape[1]
    block = 512
    rows_here = row_start + jnp.arange(row_count, dtype=jnp.int32)
    cols_here = jnp.arange(col_count, dtype=jnp.int32)

    def add_block(index, acc):
        piece = lax.dynamic_slice_in_dim(table, index * block, block, 1)
        first_x, last_x, first_y, last_y, count = (piece[0], piece[1], piece[2], piece[3], piece[4])
        span_x = (last_x - first_x + 1).astype(jnp.float32)
        span_y = (last_y - first_y + 1).astype(jnp.float32)
        weight = (
            jnp.log(count.astype(jnp.float32)) * (span_x + span_y) / (span_x * span_y)
        ).astype(jnp.bfloat16)
        row_hits = (
            (rows_here[None, :] >= first_y[:, None]) & (rows_here[None, :] <= last_y[:, None])
        ).astype(jnp.bfloat16)
        col_hits = (cols_here[None, :] >= first_x[:, None]) & (
            cols_here[None, :] <= last_x[:, None]
        )
        weighted = jnp.where(col_hits, weight[:, None], jnp.zeros((), jnp.bfloat16))
        return acc + lax.dot_general(
            row_hits, weighted, (((0,), (0,)), ((), ())), preferred_element_type=jnp.float32
        )

    empty = jnp.zeros((row_count, col_count), jnp.float32)
    return lax.fori_loop(0, total_nets // block, add_block, empty)


def per_device(boxes, pins, capacity, cell_bin, cell_area):
    tile_rows, tile_cols = capacity.shape
    row_start = lax.axis_index(ROW) * tile_rows
    table = jnp.concatenate([boxes, pins[None, :]], axis=0)
    band = raster(table, row_start, tile_rows, tile_cols * lax.axis_size(COL))
    rudy = lax.psum_scatter(band, COL, scatter_dimension=1, tiled=True)
    excess = jnp.maximum(rudy - capacity, 0.0)
    ladder = jnp.arange(tile_rows, dtype=jnp.int32)
    lower = (ladder[:, None] >= ladder[None, :]).astype(jnp.float32)
    within = jnp.dot(
        lower, excess, precision=lax.Precision.HIGHEST, preferred_element_type=jnp.float32
    )
    column_sum = within[-1]
    stacked = collect(column_sum[None, :], ROW, 0)
    above = jnp.arange(stacked.shape[0], dtype=jnp.int32) < lax.axis_index(ROW)
    carried = jnp.sum(jnp.where(above[:, None], stacked, 0.0), axis=0)
    prefix = within + carried[None, :]
    grid_rows = tile_rows * lax.axis_size(ROW)
    inflation = 1.0 + 2.0 * prefix / grid_rows
    looked = jnp.take(inflation.reshape(-1), cell_bin[0], axis=0)
    grown = cell_area * looked[None, :]
    area_sum, grown_sum = (
        one_axis_at_a_time(jnp.sum(cell_area), ROW_COL),
        one_axis_at_a_time(jnp.sum(grown), ROW_COL),
    )
    cell_sizes = grown * (area_sum / grown_sum)
    return (rudy, inflation, cell_sizes)


def solution(mesh):
    split = Mesh(mesh.devices.reshape(4, 2, 8, 2, 2), ("row_0", "row_1", "col_0", "col_1", "col_2"))
    placed = (P(None, COL), P(COL), P(ROW, COL), P(ROW, COL), P(ROW, COL))
    return jax.shard_map(
        per_device,
        mesh=split,
        in_specs=placed,
        out_specs=(P(ROW, COL), P(ROW, COL), P(ROW, COL)),
        check_vma=False,
    )
```

profile of v0, /device:TPU:1, one launch (start us, length us, event | category | flops | bytes accessed | tf_op | source)
XLA Modules:
  0.0 262.5 jit_solution(17198931388420724391)
XLA Ops:
  7.2 0.0 reduce-scatter.2.cloned.1.call-start
  7.2 0.8 pad_add_fusion
  8.0 40.2 %while.15 = (s32[]{:T(128)}, f32[512,4096]{1,0:T(8,128)}, s32[5,2048]{1,0:T(8,128)S(1)}, s32[]{:T(128)}, s32[]{:T(128)}, /*index=5*/s32[]{:T(128)}, s32[]{}, s32[]{:T(128)}, s32[]{:T(128)}, s32[]{}, /*index=10*/s32[]{}, s32[]{}) while((s32[]{:T(128)}, f32[512,4096]{1,0:T(8,128)}, s32[5,2048]{1,0:T(8,128)S(1)}, ...), condition=%wide.region_1.2_spmd.clone.clone, body=%wide.region_0.1_spmd.clone.clone.sunk | while | flops 2160859648 | bytes 16822520 | solution.py:61
  8.0 0.1 fusion.37
  8.1 0.1 fusion.38
  8.3 7.3 %select_add_fusion.2 = f32[512,4096]{1,0:T(8,128)} fusion(f32[512,4096]{1,0:T(8,128)} %get-tuple-element.206, s32[512]{0:T(512)S(1)} %bitcast.28, s32[512]{0:T(512)S(1)} %bitcast.30, pred[]{:T(512)S(6)} %compare.3, bf16[512]{0:T(512)(128)(2,1)S(1)} %fusion.39, s32[512]{0:T(512)S(1)} %iota_add_fusion.2, s32[512]{0:T(512)S(1)} %bitcast.32, ...), kind=kOutput, calls=%fused_computation.5.clone.1 | convolution fusion | flops 2160852992 | bytes 16788480 | tf_op jit(solution)/shard_map/while/body/eval_jaxpr/dot_general | solution.py:56
  15.6 0.1 fusion.37
  15.6 0.1 fusion.38
  15.8 10.7 %select_add_fusion.2 = f32[512,4096]{1,0:T(8,128)} fusion(f32[512,4096]{1,0:T(8,128)} %get-tuple-element.206, s32[512]{0:T(512)S(1)} %bitcast.28, s32[512]{0:T(512)S(1)} %bitcast.30, pred[]{:T(512)S(6)} %compare.3, bf16[512]{0:T(512)(128)(2,1)S(1)} %fusion.39, s32[512]{0:T(512)S(1)} %iota_add_fusion.2, s32[512]{0:T(512)S(1)} %bitcast.32, ...), kind=kOutput, calls=%fused_computation.5.clone.1 | convolution fusion | flops 2160852992 | bytes 16788480 | tf_op jit(solution)/shard_map/while/body/eval_jaxpr/dot_general | solution.py:56
  26.5 0.1 fusion.37
  26.5 0.1 fusion.38
  26.7 10.7 %select_add_fusion.2 = f32[512,4096]{1,0:T(8,128)} fusion(f32[512,4096]{1,0:T(8,128)} %get-tuple-element.206, s32[512]{0:T(512)S(1)} %bitcast.28, s32[512]{0:T(512)S(1)} %bitcast.30, pred[]{:T(512)S(6)} %compare.3, bf16[512]{0:T(512)(128)(2,1)S(1)} %fusion.39, s32[512]{0:T(512)S(1)} %iota_add_fusion.2, s32[512]{0:T(512)S(1)} %bitcast.32, ...), kind=kOutput, calls=%fused_computation.5.clone.1 | convolution fusion | flops 2160852992 | bytes 16788480 | tf_op jit(solution)/shard_map/while/body/eval_jaxpr/dot_general | solution.py:56
  37.3 0.1 fusion.37
  37.4 0.1 fusion.38
  37.5 10.7 %select_add_fusion.2 = f32[512,4096]{1,0:T(8,128)} fusion(f32[512,4096]{1,0:T(8,128)} %get-tuple-element.206, s32[512]{0:T(512)S(1)} %bitcast.28, s32[512]{0:T(512)S(1)} %bitcast.30, pred[]{:T(512)S(6)} %compare.3, bf16[512]{0:T(512)(128)(2,1)S(1)} %fusion.39, s32[512]{0:T(512)S(1)} %iota_add_fusion.2, s32[512]{0:T(512)S(1)} %bitcast.32, ...), kind=kOutput, calls=%fused_computation.5.clone.1 | convolution fusion | flops 2160852992 | bytes 16788480 | tf_op jit(solution)/shard_map/while/body/eval_jaxpr/dot_general | solution.py:56
  48.2 0.0 copy-start.1
  48.2 0.0 copy-start
  48.2 0.0 copy-start.2
  48.2 0.0 reduce-scatter.2.cloned.1.call-update
  48.3 0.7 copy-done.1
  49.0 131.8 %reduce-scatter.2.cloned.1.call-done = f32[512,128]{1,0:T(8,128)} async-done(((f32[512,4096]{1,0:T(8,128)}), f32[512,128]{1,0:T(8,128)}) %reduce-scatter.2.cloned.1.call-update) | async-done | bytes 262160 | tf_op jit(solution)/shard_map/reduce_scatter | solution.py:69
  180.7 0.0 copy-done
  180.7 1.6 fusion.20
  182.3 0.6 broadcast_in_dim.77
  182.9 6.0 %all-to-all-start = ((f32[8,1,128]{2,1,0:T(1,128)}), f32[8,1,128]{2,1,0:T(1,128)S(1)}, u32[]{:S(2)}, u32[]{:S(2)}) async-start(f32[8,1,128]{2,1,0:T(1,128)} %broadcast_in_dim.77), calls=%async_computation.1 | async-start | bytes 8192 | tf_op jit(solution)/shard_map/all_to_all | solution.py:22
  189.0 6.4 %all-to-all-done = f32[8,1,128]{2,1,0:T(1,128)S(1)} async-done(((f32[8,1,128]{2,1,0:T(1,128)}), f32[8,1,128]{2,1,0:T(1,128)S(1)}, u32[]{:S(2)}, u32[]{:S(2)}) %all-to-all-start) | async-done | bytes 4128 | tf_op jit(solution)/shard_map/all_to_all | solution.py:22
  195.4 0.1 select_reduce_fusion
  195.5 0.7 multiply_add_fusion
  196.3 11.8 %gather_fusion = f32[2048]{0:T(1024)S(1)} fusion(f32[65536]{0:T(1024)S(1)} %fusion.29, s32[2048]{0:T(1024)S(1)} %broadcast_clamp_fusion), kind=kCustom, calls=%fused_computation | custom fusion | bytes 24576 | tf_op jit(solution)/shard_map/jit(_take)/gather | solution.py:83
  208.0 0.0 copy-done.2
  208.1 0.6 fusion.26
  208.7 7.6 %all-reduce.1 = (f32[]{:T(128)}, f32[]{:T(128)}) all-reduce(f32[]{:T(128)} %get-tuple-element.159, f32[]{:T(128)} %get-tuple-element.153), channel_id=1, replica_groups=mesh['row_0'=4,'row_1'=2,'col_0'=8,'col_1'=2,'col_2'=2] {'row_0'}, use_global_device_ids=true, to_apply=%region_5.6 | all-reduce | flops 2 | bytes 16 | tf_op jit(solution)/shard_map/psum | solution.py:32
  216.3 5.9 %all-reduce.4 = (f32[]{:T(128)}, f32[]{:T(128)}) all-reduce(f32[]{:T(128)} %get-tuple-element.145, f32[]{:T(128)} %get-tuple-element.146), channel_id=1, replica_groups=mesh['row_0'=4,'row_1'=2,'col_0'=8,'col_1'=2,'col_2'=2] {'row_1'}, use_global_device_ids=true, to_apply=%region_6.7 | all-reduce | flops 2 | bytes 16 | tf_op jit(solution)/shard_map/psum | solution.py:32
  222.1 12.6 %all-reduce = (f32[]{:T(128)}, f32[]{:T(128)}) all-reduce(f32[]{:T(128)} %get-tuple-element.151, f32[]{:T(128)} %get-tuple-element.152), channel_id=1, replica_groups=mesh['row_0'=4,'row_1'=2,'col_0'=8,'col_1'=2,'col_2'=2] {'col_0'}, use_global_device_ids=true, to_apply=%region_7.8 | all-reduce | flops 2 | bytes 16 | tf_op jit(solution)/shard_map/psum | solution.py:32
  234.8 6.5 %all-reduce.3 = (f32[]{:T(128)}, f32[]{:T(128)}) all-reduce(f32[]{:T(128)} %get-tuple-element.143, f32[]{:T(128)} %get-tuple-element.144), channel_id=1, replica_groups=mesh['row_0'=4,'row_1'=2,'col_0'=8,'col_1'=2,'col_2'=2] {'col_1'}, use_global_device_ids=true, to_apply=%region_8.9 | all-reduce | flops 2 | bytes 16 | tf_op jit(solution)/shard_map/psum | solution.py:32
  241.3 12.4 %all-reduce.2 = (f32[]{:T(128)}, f32[]{:T(128)}) all-reduce(f32[]{:T(128)} %get-tuple-element.149, f32[]{:T(128)} %get-tuple-element.150), channel_id=1, replica_groups=mesh['row_0'=4,'row_1'=2,'col_0'=8,'col_1'=2,'col_2'=2] {'col_2'}, use_global_device_ids=true, to_apply=%region_9.10 | all-reduce | flops 2 | bytes 16 | tf_op jit(solution)/shard_map/psum | solution.py:32
  255.1 0.6 broadcast_multiply_fusion
  (14 shorter events, 0.1 us)
Async XLA Ops:
  7.2 173.6 %reduce-scatter.2.cloned.1.call-start = ((), (), s32[]{:S(2)}) async-start(), calls=%async_computation.2 | async-start | bytes 8650752 | tf_op jit(solution)/shard_map/reduce_scatter | solution.py:69
  48.2 0.7 copy-start.1
  48.2 132.5 %copy-start = (f32[512,128]{1,0:T(8,128)S(1)}, f32[512,128]{1,0:T(8,128)}, u32[]{:S(2)}) copy-start(f32[512,128]{1,0:T(8,128)} %param.9) | copy-start | bytes 786436
  48.2 159.8 %copy-start.2 = (f32[1,2048]{1,0:T(1,128)S(1)}, f32[1,2048]{1,0:T(1,128)}, u32[]{:S(2)}) copy-start(f32[1,2048]{1,0:T(1,128)} %param.11) | copy-start | bytes 24580
  182.9 12.5 %all-to-all-start = ((f32[8,1,128]{2,1,0:T(1,128)}), f32[8,1,128]{2,1,0:T(1,128)S(1)}, u32[]{:S(2)}, u32[]{:S(2)}) async-start(f32[8,1,128]{2,1,0:T(1,128)} %broadcast_in_dim.77), calls=%async_computation.1 | async-start | bytes 8192 | tf_op jit(solution)/shard_map/all_to_all | solution.py:22
Sparse Core Ops, SparseCore 0:
  48.4 132.3 reduce-scatter.1
where the time goes:
time: 263 us
  waiting for transfers between devices  138 us (52%)
  blocking collectives  45 us (17%)
  matrix products  40.9 us (16%)
  between operations  15.5 us (6%)
  local copies, waits for them, and re-layouts  13.4 us (5%)
  starting transfers between devices  6.08 us (2%)
  other arithmetic  3.3 us (1%)
    reduce_scatter x1, waiting for transfers between devices, per_device(): rudy = lax.psum_scatter(band, COL, scatter_dimension=1, tiled=True)  132 us
    psum x5, blocking collectives, one_axis_at_a_time(): return functools.reduce(lax.psum, axes, shard)  45 us
    dot_general x4, matrix products, add_block(): lax.dot_general(row_hits, weighted, (((0,), (0,)), ((), ())), preferred_e...  39.4 us
    gather x1, local copies, waits for them, and re-layouts, per_device(): looked = jnp.take(inflation.reshape(-1), cell_bin[0], axis=0)  11.8 us
    all_to_all x1, waiting for transfers between devices, copy_for_each(): lax.all_to_all(jnp.broadcast_to(shard[None], (peers, *shard.shape)), axis...  6.45 us
    all_to_all x1, starting transfers between devices, copy_for_each(): lax.all_to_all(jnp.broadcast_to(shard[None], (peers, *shard.shape)), axis...  6.04 us
  transfers between devices with their start and end apart: 2, of which 2 were waited for; matrix products, arithmetic and copies ran while one was open for 0% of the time, Pallas kernels for 0%

commit v1 on v0

v1 whole, which is shorter than its diff:
```python
import functools

import jax
import jax.numpy as jnp
from jax import lax
from jax.experimental import pallas as pl
from jax.experimental.pallas import tpu as pltpu
from jax.sharding import PartitionSpec as P

MESH = pl.DeviceIdType.MESH
F32 = jnp.float32
BF16 = jnp.bfloat16
SLOTS = 80
HALF_SLOTS = 256
LANES = 128


def iota(shape, dim, dtype=F32):
    return lax.broadcasted_iota(jnp.int32, shape, dim).astype(dtype)


def ones_where(mask, dtype=BF16):
    return jnp.where(mask, jnp.ones((), dtype), jnp.zeros((), dtype))


def dot(a, b):
    return lax.dot_general(a, b, (((1,), (0,)), ((), ())), preferred_element_type=F32)


def dot_nt(a, b):
    return lax.dot_general(a, b, (((1,), (1,)), ((), ())), preferred_element_type=F32)


def split2(x):
    hi = x.astype(BF16)
    return hi, (x - hi.astype(F32)).astype(BF16)


def sparse_kernel(
    n_row, n_col,
    boxes_h, pins_h, cap_h, cbin_h, area_h,
    rudy_h, infl_h, sizes_h, flag_h,
    boxes, pins, cap, cbin, area, rudy, infl, sizes, flag,
    feat, hits, send, recv, onehot, early_s, early_r, mid_s, mid_r, fin_s, fin_r,
    in_sem, out_sem, a2a_ss, a2a_rs, early_ss, early_rs, mid_ss, mid_rs, fin_ss, fin_rs,
):
    row = lax.axis_index("row")
    col = lax.axis_index("col")
    tile_r, tile_c = cap.shape
    nets = pins.shape[1]
    cells = cbin.shape[1]
    chunks = nets // LANES
    half = nets // 2

    loads = [
        pltpu.make_async_copy(src, dst, in_sem.at[i])
        for i, (src, dst) in enumerate(
            ((boxes_h, boxes), (pins_h, pins), (cbin_h, cbin), (area_h, area), (cap_h, cap))
        )
    ]
    for load in loads:
        load.start()

    barrier = pltpu.get_barrier_semaphore()
    col_steps = sorted(range(1, n_col), key=lambda o: -min(o, n_col - o))
    for step in col_steps:
        pl.semaphore_signal(
            barrier, inc=1, device_id={"col": lax.rem(col + step, n_col)}, device_id_type=MESH
        )
    for step in range(1, n_row):
        pl.semaphore_signal(
            barrier, inc=1, device_id={"row": lax.rem(row + step, n_row)}, device_id_type=MESH
        )

    loads[0].wait()
    loads[1].wait()
    x0, x1, y0, y1 = (boxes[i : i + 1, :] for i in range(4))
    dx = (x1 - x0 + 1).astype(F32)
    dy = (y1 - y0 + 1).astype(F32)
    weight = jnp.log(pins[...].astype(F32)) * (dx + dy) / (dx * dy)
    weight = weight.astype(BF16).astype(F32)
    row_start = row * tile_r
    y_first = jnp.clip(y0 - row_start, 0, tile_r)
    y_end = jnp.clip(y1 + 1 - row_start, 0, tile_r)
    in_band = jnp.where(y_end > y_first, 1.0, 0.0).astype(F32)
    x_end = x1 + 1
    zero_row = jnp.zeros((1, nets), F32)
    parts = [
        (x0 & -LANES).astype(F32), (x_end & -LANES).astype(F32),
        (y_first & -256).astype(F32), (y_end & -256).astype(F32),
        weight, zero_row, zero_row, zero_row,
        (x0 & (LANES - 1)).astype(F32), (x_end & (LANES - 1)).astype(F32),
        (y_first & 255).astype(F32), (y_end & 255).astype(F32),
        zero_row, zero_row, zero_row, zero_row,
    ]
    for i, part in enumerate(parts):
        feat[i : i + 1, :] = part
    for j in range(chunks):
        hits[j : j + 1, :] = in_band[:, j * LANES : (j + 1) * LANES]
    table = feat[...].astype(BF16)
    member = hits[...].astype(BF16)
    ci, cj = iota((chunks, chunks), 0), iota((chunks, chunks), 1)
    per_half = chunks // 2
    same_half = jnp.where(ci >= per_half, 1.0, 0.0) == jnp.where(cj >= per_half, 1.0, 0.0)
    ahead = dot(ones_where((ci > cj) & same_half), member)
    before = ones_where(iota((LANES, LANES), 0) < iota((LANES, LANES), 1))
    place = dot(member, before) + dot(ahead.astype(BF16), jnp.ones((LANES, LANES), BF16))
    longest = jnp.max(place + hits[...], keepdims=True)
    place = jnp.where((hits[...] > 0.0) & (place < HALF_SLOTS), place, -1.0).astype(BF16)
    slot = iota((HALF_SLOTS, LANES), 0, BF16)
    packed = []
    for h in range(2):
        pick = jnp.concatenate(
            [
                ones_where(slot == jnp.broadcast_to(place[j : j + 1, :], slot.shape))
                for j in range(h * per_half, (h + 1) * per_half)
            ],
            axis=1,
        )
        packed.append(dot_nt(pick, table[:, h * half : (h + 1) * half]).T)
    packed = jnp.concatenate(packed, axis=1)
    listed = packed[0:8] + packed[8:16]
    band_slots = 2 * HALF_SLOTS

    tile_x = iota((n_col, band_slots), 0) * tile_c
    meets = (listed[0:1] < tile_x + tile_c) & (listed[1:2] > tile_x)
    wide = band_slots + LANES
    ti, tj = iota((band_slots, wide), 0), iota((band_slots, wide), 1)
    counted = dot(ones_where(meets), ones_where((ti < tj) | (tj >= band_slots)))
    order = counted[:, :band_slots]
    count = jnp.where(longest > HALF_SLOTS, 1e6, counted[:, band_slots:])
    odd = lax.rem(col, 2).astype(F32)
    order = jnp.where(meets, odd * (SLOTS - 1) + (1.0 - 2.0 * odd) * order, -1.0).astype(BF16)
    slot = iota((SLOTS, band_slots), 0, BF16)
    pick = jnp.concatenate(
        [
            ones_where(slot == jnp.broadcast_to(order[d : d + 1, :], slot.shape))
            for d in range(n_col)
        ],
        axis=0,
    )
    taken = dot_nt(pick, packed.astype(BF16))
    pad = jnp.zeros((LANES - SLOTS, 16), F32)
    line = lax.broadcasted_iota(jnp.int32, (8, LANES), 0)
    for d in range(n_col):
        block = jnp.concatenate([taken[d * SLOTS : (d + 1) * SLOTS], pad], axis=0).T
        send[d] = jnp.where(line == 5, count[d : d + 1, :], block[0:8] + block[8:16])

    pl.semaphore_wait(barrier, n_col - 1 + n_row - 1)
    started = []
    for step in col_steps:
        peer = lax.rem(col + step, n_col)
        copy = pltpu.make_async_remote_copy(
            src_ref=send.at[peer], dst_ref=recv.at[col],
            send_sem=a2a_ss.at[peer], recv_sem=a2a_rs.at[col],
            device_id={"col": peer}, device_id_type=MESH,
        )
        copy.start()
        started.append(copy)
    recv[col] = send[col]

    loads[2].wait()
    loads[3].wait()
    bins = cbin[...]
    bin_row = (bins // tile_c).astype(F32)
    bin_col = (bins % tile_c).astype(F32)
    for h in range(tile_r // 256):
        onehot[h * 256 : (h + 1) * 256, :] = ones_where(
            iota((256, cells), 0, BF16)
            == jnp.broadcast_to((bin_row - 256.0 * h).astype(BF16), (256, cells))
        )
    in_col = iota((tile_c, cells), 0, BF16) == jnp.broadcast_to(bin_col.astype(BF16), (tile_c, cells))
    area_hi, area_lo = split2(area[...])
    nought = jnp.zeros((), BF16)
    by_col = jnp.concatenate(
        [
            jnp.where(in_col, jnp.broadcast_to(area_hi, (tile_c, cells)), nought),
            jnp.where(in_col, jnp.broadcast_to(area_lo, (tile_c, cells)), nought),
        ],
        axis=0,
    )
    bin_area = dot_nt(onehot[...], by_col)
    bin_area = bin_area[:, :tile_c] + bin_area[:, tile_c:]
    early_s[...] = jnp.sum(bin_area, axis=0, keepdims=True)
    for step in range(1, n_row):
        peer = lax.rem(row + step, n_row)
        copy = pltpu.make_async_remote_copy(
            src_ref=early_s, dst_ref=early_r.at[row],
            send_sem=early_ss.at[peer], recv_sem=early_rs.at[row],
            device_id={"row": peer}, device_id_type=MESH,
        )
        copy.start()
        started.append(copy)
    early_r[row] = early_s[...]

    for step in reversed(col_steps):
        peer = lax.rem(col + step, n_col)
        pltpu.make_async_remote_copy(
            src_ref=send.at[peer], dst_ref=recv.at[peer],
            send_sem=a2a_ss.at[peer], recv_sem=a2a_rs.at[peer],
            device_id={"col": peer}, device_id_type=MESH,
        ).wait_recv()
    merged = []
    over = jnp.zeros((1, LANES), F32)
    for p in range(n_col // 2):
        even = recv[2 * p]
        odds = pltpu.roll(recv[2 * p + 1], LANES - SLOTS, 1)
        merged.append(even + odds)
        n_even, n_odd = even[5:6], odds[5:6]
        spilt = (n_even > SLOTS) | (n_odd > SLOTS) | (n_even + n_odd > LANES)
        over = over + jnp.where(spilt, 1.0, 0.0)
    merged = jnp.concatenate(merged, axis=1)
    total = merged.shape[1]
    shift = (col * tile_c).astype(F32)
    x_lo = jnp.clip(merged[0:1] - shift, 0.0, 1.0 * tile_c).astype(BF16)
    x_hi = jnp.clip(merged[1:2] - shift, 0.0, 1.0 * tile_c).astype(BF16)
    lane = iota((tile_c, total), 0, BF16)
    full = lambda x, n: jnp.broadcast_to(x, (n, total))
    col_weight = jnp.where(
        (lane >= full(x_lo, tile_c)) & (lane < full(x_hi, tile_c)),
        full(merged[4:5].astype(BF16), tile_c), nought,
    )
    lane = iota((256, total), 0, BF16)
    for h in range(tile_r // 256):
        y_lo = jnp.clip(merged[2:3] - 256.0 * h, 0.0, 256.0).astype(BF16)
        y_hi = jnp.clip(merged[3:4] - 256.0 * h, 0.0, 256.0).astype(BF16)
        row_hit = ones_where((lane >= full(y_lo, 256)) & (lane < full(y_hi, 256)))
        rudy[h * 256 : (h + 1) * 256, :] = dot_nt(row_hit, col_weight)
    stores = [pltpu.make_async_copy(rudy, rudy_h, out_sem.at[0])]
    stores[0].start()

    loads[4].wait()
    excess = jnp.maximum(rudy[...] - cap[...], 0.0)
    e_hi, e_lo = split2(excess)
    lower = ones_where(iota((tile_r, tile_r), 0) >= iota((tile_r, tile_r), 1))
    within = dot(lower, jnp.concatenate([e_hi, e_lo], axis=1))
    within = within[:, :tile_c] + within[:, tile_c:]
    mid_s[0:1, :] = within[tile_r - 1 : tile_r]
    mid_s[1:2, :] = jnp.sum(bin_area * within, axis=0, keepdims=True)
    mid_s[2:3, :] = over
    mid_s[3:4, :] = over
    for step in range(1, n_row):
        peer = lax.rem(row + step, n_row)
        copy = pltpu.make_async_remote_copy(
            src_ref=mid_s, dst_ref=mid_r.at[row],
            send_sem=mid_ss.at[peer], recv_sem=mid_rs.at[row],
            device_id={"row": peer}, device_id_type=MESH,
        )
        copy.start()
        started.append(copy)
    mid_r[row] = mid_s[...]
    for step in range(1, n_row):
        peer = lax.rem(row + step, n_row)
        for src, dst, ss, rs in (
            (early_s, early_r, early_ss, early_rs), (mid_s, mid_r, mid_ss, mid_rs)
        ):
            pltpu.make_async_remote_copy(
                src_ref=src, dst_ref=dst.at[peer], send_sem=ss.at[peer], recv_sem=rs.at[peer],
                device_id={"row": peer}, device_id_type=MESH,
            ).wait_recv()
    factor = 2.0 / (tile_r * n_row)
    running = jnp.zeros((1, tile_c), F32)
    carried = jnp.zeros((1, tile_c), F32)
    areas = jnp.zeros((1, tile_c), F32)
    growth = jnp.zeros((1, tile_c), F32)
    over = jnp.zeros((1, tile_c), F32)
    for r in range(n_row):
        got = mid_r[r]
        col_area = early_r[r]
        carried = jnp.where(row == r, running, carried)
        areas = areas + col_area
        growth = growth + got[1:2] + running * col_area
        running = running + got[0:1]
        over = over + got[2:3]
    fin_s[0:1, :] = areas + factor * growth
    fin_s[1:2, :] = areas
    fin_s[2:3, :] = over
    fin_s[3:4, :] = over
    for step in col_steps:
        peer = lax.rem(col + step, n_col)
        copy = pltpu.make_async_remote_copy(
            src_ref=fin_s, dst_ref=fin_r.at[col],
            send_sem=fin_ss.at[peer], recv_sem=fin_rs.at[col],
            device_id={"col": peer}, device_id_type=MESH,
        )
        copy.start()
        started.append(copy)
    fin_r[col] = fin_s[...]

    inflation = 1.0 + factor * (within + carried)
    infl[...] = inflation
    stores.append(pltpu.make_async_copy(infl, infl_h, out_sem.at[1]))
    stores[1].start()
    i_hi, i_lo = split2(inflation.T)
    looked = dot(jnp.concatenate([i_hi, i_lo], axis=0), onehot[...])
    looked = looked[:tile_c] + looked[tile_c:]
    in_col = iota((tile_c, cells), 0) == jnp.broadcast_to(bin_col, (tile_c, cells))
    looked = jnp.sum(jnp.where(in_col, looked, 0.0), axis=0, keepdims=True)
    grown = area[...] * looked

    for step in reversed(col_steps):
        peer = lax.rem(col + step, n_col)
        pltpu.make_async_remote_copy(
            src_ref=fin_s, dst_ref=fin_r.at[peer], send_sem=fin_ss.at[peer], recv_sem=fin_rs.at[peer],
            device_id={"col": peer}, device_id_type=MESH,
        ).wait_recv()
    totals = fin_r[0]
    for c in range(1, n_col):
        totals = totals + fin_r[c]
    totals = jnp.sum(totals, axis=1, keepdims=True)
    sizes[...] = grown * (totals[1:2] / totals[0:1])
    flag[...] = jnp.broadcast_to(totals[2:3], flag.shape)
    stores.append(pltpu.make_async_copy(sizes, sizes_h, out_sem.at[2]))
    stores.append(pltpu.make_async_copy(flag, flag_h, out_sem.at[3]))
    for store in stores[2:]:
        store.start()
    for copy in started:
        copy.wait_send()
    for store in stores:
        store.wait()


def sparse_program(n_row, n_col, boxes, pins, capacity, cell_bin, cell_area):
    tile_r, tile_c = capacity.shape
    nets = pins.shape[0]
    cells = cell_bin.shape[1]
    vm = pltpu.VMEM
    dma = pltpu.SemaphoreType.DMA
    anywhere = pl.BlockSpec(memory_space=pl.ANY)
    shape = jax.ShapeDtypeStruct
    return pl.pallas_call(
        functools.partial(sparse_kernel, n_row, n_col),
        name="nets_to_tiles",
        out_shape=(
            shape((tile_r, tile_c), F32), shape((tile_r, tile_c), F32),
            shape((1, cells), F32), shape((1, LANES), F32),
        ),
        in_specs=[anywhere] * 5,
        out_specs=(anywhere,) * 4,
        scratch_shapes=[
            vm((4, nets), jnp.int32), vm((1, nets), jnp.int32), vm((tile_r, tile_c), F32),
            vm((1, cells), jnp.int32), vm((1, cells), F32),
            vm((tile_r, tile_c), F32), vm((tile_r, tile_c), F32), vm((1, cells), F32),
            vm((1, LANES), F32),
            vm((16, nets), F32), vm((nets // LANES, LANES), F32),
            vm((n_col, 8, LANES), F32), vm((n_col, 8, LANES), F32),
            vm((tile_r, cells), BF16),
            vm((1, tile_c), F32), vm((n_row, 1, tile_c), F32),
            vm((4, tile_c), F32), vm((n_row, 4, tile_c), F32),
            vm((4, tile_c), F32), vm((n_col, 4, tile_c), F32),
            dma((5,)), dma((4,)),
            dma((n_col,)), dma((n_col,)), dma((n_row,)), dma((n_row,)),
            dma((n_row,)), dma((n_row,)), dma((n_col,)), dma((n_col,)),
        ],
        compiler_params=pltpu.CompilerParams(
            collective_id=0, has_side_effects=True, vmem_limit_bytes=40 * 1024 * 1024
        ),
    )(boxes, pins.reshape(1, nets), capacity, cell_bin, cell_area)


def to_everyone(shard, axis):
    peers = lax.axis_size(axis)
    return lax.all_to_all(
        jnp.broadcast_to(shard[None], (peers, *shard.shape)), axis, 0, 0, tiled=True
    )


def dense_program(boxes, pins, capacity, cell_bin, cell_area):
    tile_rows, tile_cols = capacity.shape
    table = jnp.concatenate([boxes, pins[None, :]], axis=0)
    table = to_everyone(table, "col")
    rows_here = lax.axis_index("row") * tile_rows + jnp.arange(tile_rows, dtype=jnp.int32)
    cols_here = lax.axis_index("col") * tile_cols + jnp.arange(tile_cols, dtype=jnp.int32)

    def add_block(index, acc):
        first_x, last_x, first_y, last_y, pin = table[index]
        span_x = (last_x - first_x + 1).astype(F32)
        span_y = (last_y - first_y + 1).astype(F32)
        weight = jnp.log(pin.astype(F32)) * (span_x + span_y) / (span_x * span_y)
        row_hits = (rows_here[:, None] >= first_y[None, :]) & (rows_here[:, None] <= last_y[None, :])
        col_hits = (cols_here[:, None] >= first_x[None, :]) & (cols_here[:, None] <= last_x[None, :])
        weighted = jnp.where(col_hits, weight.astype(BF16)[None, :], jnp.zeros((), BF16))
        return acc + dot_nt(row_hits.astype(BF16), weighted)

    rudy = lax.fori_loop(
        0, table.shape[0], add_block, jnp.zeros((tile_rows, tile_cols), F32)
    )
    excess = jnp.maximum(rudy - capacity, 0.0)
    ladder = jnp.arange(tile_rows, dtype=jnp.int32)
    lower = (ladder[:, None] >= ladder[None, :]).astype(F32)
    within = jnp.dot(
        lower, excess, precision=lax.Precision.HIGHEST, preferred_element_type=F32
    )
    sums = to_everyone(within[-1][None, :], "row")[:, 0]
    above = jnp.arange(sums.shape[0], dtype=jnp.int32) < lax.axis_index("row")
    carried = jnp.sum(jnp.where(above[:, None], sums, 0.0), axis=0)
    inflation = 1.0 + 2.0 * (within + carried[None, :]) / (tile_rows * lax.axis_size("row"))
    looked = jnp.take(inflation.reshape(-1), cell_bin[0], axis=0)
    grown = cell_area * looked[None, :]
    totals = jnp.stack([jnp.sum(cell_area), jnp.sum(grown)])[None, :]
    for axis in ("row", "col"):
        totals = jnp.sum(to_everyone(totals, axis), axis=0)
    cell_sizes = grown * (totals[0, 0] / totals[0, 1])
    return rudy, inflation, cell_sizes


def per_device(n_row, n_col, *args):
    rudy, inflation, cell_sizes, flag = sparse_program(n_row, n_col, *args)

    def again(state):
        held = [jnp.where(state[3][0, 0] > 0.0, x, jnp.ones((), x.dtype)) for x in args]
        return (*dense_program(*held), jnp.zeros_like(flag))

    state = lax.while_loop(
        lambda state: state[3][0, 0] > 0.0, again, (rudy, inflation, cell_sizes, flag)
    )
    return state[:3]


def solution(mesh):
    n_row, n_col = mesh.shape["row"], mesh.shape["col"]
    placed = (P(None, "col"), P("col"), P("row", "col"), P("row", "col"), P("row", "col"))
    return jax.shard_map(
        functools.partial(per_device, n_row, n_col),
        mesh=mesh,
        in_specs=placed,
        out_specs=(P("row", "col"),) * 3,
        check_vma=False,
    )
```

time: 263 us -> 36.8 us (0.14)
  waiting for transfers between devices: 138 us -> 0 us
  blocking collectives: 45 us -> 0 us
  matrix products: 40.9 us -> 0 us
  Pallas kernels: 0 us -> 30.8 us
  between operations: 15.5 us -> 0.65 us
  local copies, waits for them, and re-layouts: 13.4 us -> 4.63 us
  starting transfers between devices: 6.08 us -> 0 us
  other arithmetic: 3.3 us -> 0 us
    reduce_scatter x1 -> x0, waiting for transfers between devices: 132 us -> none  [per_device(): rudy = lax.psum_scatter(band, COL, scatter_dimension=1, tiled=True)]
    psum x5 -> x0, blocking collectives: 45 us -> none  [one_axis_at_a_time(): return functools.reduce(lax.psum, axes, shard)]
    dot_general x5 -> x0, matrix products: 40.9 us -> none  [the longest x4 39.4 us: add_block(): lax.dot_general(row_hits, weighted, (((0,), (0,)), ((), ())), preferred_e...]
    pallas_call x0 -> x1, Pallas kernels: none -> 30.8 us  [sparse_program(): pl.pallas_call(functools.partial(sparse_kernel, n_row, n_col), name='nets...]
    gather x1 -> x0, local copies, waits for them, and re-layouts: 11.8 us -> none  [per_device(): looked = jnp.take(inflation.reshape(-1), cell_bin[0], axis=0)]
    all_to_all x1 -> x0, waiting for transfers between devices: 6.45 us -> none  [copy_for_each(): lax.all_to_all(jnp.broadcast_to(shard[None], (peers, *shard.shape)), axis...]
    all_to_all x1 -> x0, starting transfers between devices: 6.04 us -> none  [copy_for_each(): lax.all_to_all(jnp.broadcast_to(shard[None], (peers, *shard.shape)), axis...]
    unnamed x6 -> x3, local copies, waits for them, and re-layouts: 0.68 us -> 4.63 us
  transfers between devices with their start and end apart: 2 -> 0, of which waited for: 2 -> 0; matrix products, arithmetic and copies ran while one was open for 0% -> 0% of each run, Pallas kernels for 0% -> 0%
where the time goes in v1:
time: 36.8 us; the launch traced here: 36.6 us
  Pallas kernels  30.8 us (84%)
  local copies, waits for them, and re-layouts  4.63 us (13%)
  between operations  0.65 us (2%)
  loops' own time  0.56 us (2%)
    pallas_call x1, Pallas kernels, sparse_program(): pl.pallas_call(functools.partial(sparse_kernel, n_row, n_col), name='nets...  30.8 us
    unnamed x3, local copies, waits for them, and re-layouts  4.63 us

profile of v1, /device:TPU:1, one launch (start us, length us, event | category | flops | bytes accessed | tf_op | source)
XLA Modules:
  0.0 36.6 jit_solution(3522725731668796498)
XLA Ops:
  0.6 30.8 %nets_to_tiles.1 = (f32[512,128]{1,0:T(8,128)}, f32[512,128]{1,0:T(8,128)}, f32[1,2048]{1,0:T(1,128)}, f32[1,128]{1,0:T(1,128)}) custom-call(s32[4,2048]{1,0:T(4,128)} %boxes_h.1, s32[1,2048]{1,0:T(1,128)} %bitcast.83, f32[512,128]{1,0:T(8,128)} %cap_h.1, s32[1,2048]{1,0:T(1,128)} %cbin_h.1, f32[1,2048]{1,0:T(1,128)} %area_h.1), custom_call_target="tpu_custom_call" | custom-call | tf_op jit(solution)/shard_map/nets_to_tiles/pallas_call | solution.py:331
  31.4 0.6 %while.36 = (f32[512,128]{1,0:T(8,128)}, f32[512,128]{1,0:T(8,128)}, f32[1,2048]{1,0:T(1,128)}, f32[1,128]{1,0:T(1,128)}, s32[4,2048]{1,0:T(4,128)}, /*index=5*/...) while((f32[512,128]{1,0:T(8,128)}, ...), condition=%wide.region_8.9_spmd, body=%wide.region_0.8_spmd.sunk | while | flops 676364864 | bytes 11909514 | solution.py:414
  32.0 1.7 %copy.37 = f32[512,128]{1,0:T(8,128)} copy(f32[512,128]{1,0:T(8,128)} %get-tuple-element.499) | data formatting | bytes 524288
  33.6 1.7 %copy.38 = f32[512,128]{1,0:T(8,128)} copy(f32[512,128]{1,0:T(8,128)} %get-tuple-element.500) | data formatting | bytes 524288
  35.3 1.3 %copy.39 = f32[1,2048]{1,0:T(1,128)} copy(f32[1,2048]{1,0:T(1,128)} %get-tuple-element.501) | data formatting | bytes 16384

commit v2 on v1

--- a/solution.py
+++ b/solution.py
@@ -11,6 +11,7 @@
 F32 = jnp.float32
 BF16 = jnp.bfloat16
 SLOTS = 80
+ROWS = 5
 HALF_SLOTS = 256
 LANES = 128
 
@@ -39,10 +40,10 @@
 def sparse_kernel(
     n_row, n_col,
     boxes_h, pins_h, cap_h, cbin_h, area_h,
-    rudy_h, infl_h, sizes_h, flag_h,
-    boxes, pins, cap, cbin, area, rudy, infl, sizes, flag,
+    rudy, infl, grown, totals,
+    boxes, pins, cap, cbin, area,
     feat, hits, send, recv, onehot, early_s, early_r, mid_s, mid_r, fin_s, fin_r,
-    in_sem, out_sem, a2a_ss, a2a_rs, early_ss, early_rs, mid_ss, mid_rs, fin_ss, fin_rs,
+    in_sem, a2a_ss, a2a_rs, early_ss, early_rs, mid_ss, mid_rs, fin_ss, fin_rs,
 ):
     row = lax.axis_index("row")
     col = lax.axis_index("col")
@@ -62,11 +63,14 @@
         load.start()
 
     barrier = pltpu.get_barrier_semaphore()
-    col_steps = sorted(range(1, n_col), key=lambda o: -min(o, n_col - o))
-    for step in col_steps:
-        pl.semaphore_signal(
-            barrier, inc=1, device_id={"col": lax.rem(col + step, n_col)}, device_id_type=MESH
-        )
+    chips = n_col // 2
+    chip, core = col // 2, lax.rem(col, 2)
+    far_first = sorted(range(1, chips), key=lambda o: -min(o, chips - o))
+    peers = [2 * lax.rem(chip + o, chips) + k for o in far_first for k in range(2)]
+    partner = 2 * chip + 1 - core
+    peers.append(partner)
+    for peer in peers:
+        pl.semaphore_signal(barrier, inc=1, device_id={"col": peer}, device_id_type=MESH)
     for step in range(1, n_row):
         pl.semaphore_signal(
             barrier, inc=1, device_id={"row": lax.rem(row + step, n_row)}, device_id_type=MESH
@@ -129,7 +133,7 @@
     counted = dot(ones_where(meets), ones_where((ti < tj) | (tj >= band_slots)))
     order = counted[:, :band_slots]
     count = jnp.where(longest > HALF_SLOTS, 1e6, counted[:, band_slots:])
-    odd = lax.rem(col, 2).astype(F32)
+    odd = core.astype(F32)
     order = jnp.where(meets, odd * (SLOTS - 1) + (1.0 - 2.0 * odd) * order, -1.0).astype(BF16)
     slot = iota((SLOTS, band_slots), 0, BF16)
     pick = jnp.concatenate(
@@ -142,14 +146,15 @@
     taken = dot_nt(pick, packed.astype(BF16))
     pad = jnp.zeros((LANES - SLOTS, 16), F32)
     line = lax.broadcasted_iota(jnp.int32, (8, LANES), 0)
+    lane8 = lax.broadcasted_iota(jnp.int32, (8, LANES), 1)
+    count_here = (line == 4) & (lane8 >= SLOTS)
     for d in range(n_col):
         block = jnp.concatenate([taken[d * SLOTS : (d + 1) * SLOTS], pad], axis=0).T
-        send[d] = jnp.where(line == 5, count[d : d + 1, :], block[0:8] + block[8:16])
+        send[d] = jnp.where(count_here, count[d : d + 1, :], block[0:8] + block[8:16])[0:ROWS]
 
     pl.semaphore_wait(barrier, n_col - 1 + n_row - 1)
     started = []
-    for step in col_steps:
-        peer = lax.rem(col + step, n_col)
+    for peer in peers:
         copy = pltpu.make_async_remote_copy(
             src_ref=send.at[peer], dst_ref=recv.at[col],
             send_sem=a2a_ss.at[peer], recv_sem=a2a_rs.at[col],
@@ -193,41 +198,52 @@
         started.append(copy)
     early_r[row] = early_s[...]
 
-    for step in reversed(col_steps):
-        peer = lax.rem(col + step, n_col)
+    def arrived(peer):
         pltpu.make_async_remote_copy(
             src_ref=send.at[peer], dst_ref=recv.at[peer],
             send_sem=a2a_ss.at[peer], recv_sem=a2a_rs.at[peer],
             device_id={"col": peer}, device_id_type=MESH,
         ).wait_recv()
-    merged = []
+
     over = jnp.zeros((1, LANES), F32)
-    for p in range(n_col // 2):
-        even = recv[2 * p]
-        odds = pltpu.roll(recv[2 * p + 1], LANES - SLOTS, 1)
-        merged.append(even + odds)
-        n_even, n_odd = even[5:6], odds[5:6]
-        spilt = (n_even > SLOTS) | (n_odd > SLOTS) | (n_even + n_odd > LANES)
-        over = over + jnp.where(spilt, 1.0, 0.0)
-    merged = jnp.concatenate(merged, axis=1)
-    total = merged.shape[1]
+    near_first = [0] + far_first[::-1]
+    cuts = [0, 6, 10, 14, 16] if chips == 16 else [0, chips]
     shift = (col * tile_c).astype(F32)
-    x_lo = jnp.clip(merged[0:1] - shift, 0.0, 1.0 * tile_c).astype(BF16)
-    x_hi = jnp.clip(merged[1:2] - shift, 0.0, 1.0 * tile_c).astype(BF16)
-    lane = iota((tile_c, total), 0, BF16)
-    full = lambda x, n: jnp.broadcast_to(x, (n, total))
-    col_weight = jnp.where(
-        (lane >= full(x_lo, tile_c)) & (lane < full(x_hi, tile_c)),
-        full(merged[4:5].astype(BF16), tile_c), nought,
-    )
-    lane = iota((256, total), 0, BF16)
-    for h in range(tile_r // 256):
-        y_lo = jnp.clip(merged[2:3] - 256.0 * h, 0.0, 256.0).astype(BF16)
-        y_hi = jnp.clip(merged[3:4] - 256.0 * h, 0.0, 256.0).astype(BF16)
-        row_hit = ones_where((lane >= full(y_lo, 256)) & (lane < full(y_hi, 256)))
-        rudy[h * 256 : (h + 1) * 256, :] = dot_nt(row_hit, col_weight)
-    stores = [pltpu.make_async_copy(rudy, rudy_h, out_sem.at[0])]
-    stores[0].start()
+    lane = lax.broadcasted_iota(jnp.int32, (ROWS, LANES), 1)
+    for g in range(len(cuts) - 1):
+        merged = []
+        for o in near_first[cuts[g] : cuts[g + 1]]:
+            if o == 0:
+                arrived(partner)
+            else:
+                arrived(2 * lax.rem(chip + o, chips))
+                arrived(2 * lax.rem(chip + o, chips) + 1)
+            first = 2 * lax.rem(chip + o, chips)
+            even, odds = recv[first], recv[first + 1]
+            n_even, n_odd = even[4:5], odds[4:5]
+            spilt = (n_even > SLOTS) | (n_odd > SLOTS) | (n_even + n_odd > LANES)
+            over = over + jnp.where(spilt & (lane[0:1] >= SLOTS), 1.0, 0.0)
+            even = jnp.where(lane < SLOTS, even, 0.0)
+            odds = jnp.where(lane < SLOTS, odds, 0.0)
+            merged.append(even + pltpu.roll(odds, LANES - SLOTS, 1))
+        merged = jnp.concatenate(merged, axis=1)
+        total = merged.shape[1]
+        full = lambda x, n: jnp.broadcast_to(x, (n, total))
+        x_lo = jnp.clip(merged[0:1] - shift, 0.0, 1.0 * tile_c).astype(BF16)
+        x_hi = jnp.clip(merged[1:2] - shift, 0.0, 1.0 * tile_c).astype(BF16)
+        at = iota((tile_c, total), 0, BF16)
+        col_weight = jnp.where(
+            (at >= full(x_lo, tile_c)) & (at < full(x_hi, tile_c)),
+            full(merged[4:5].astype(BF16), tile_c), nought,
+        )
+        at = iota((256, total), 0, BF16)
+        for h in range(tile_r // 256):
+            y_lo = jnp.clip(merged[2:3] - 256.0 * h, 0.0, 256.0).astype(BF16)
+            y_hi = jnp.clip(merged[3:4] - 256.0 * h, 0.0, 256.0).astype(BF16)
+            row_hit = ones_where((at >= full(y_lo, 256)) & (at < full(y_hi, 256)))
+            part = dot_nt(row_hit, col_weight)
+            rows = slice(h * 256, (h + 1) * 256)
+            rudy[rows, :] = part if g == 0 else rudy[rows, :] + part
 
     loads[4].wait()
     excess = jnp.maximum(rudy[...] - cap[...], 0.0)
@@ -238,7 +254,6 @@
     mid_s[0:1, :] = within[tile_r - 1 : tile_r]
     mid_s[1:2, :] = jnp.sum(bin_area * within, axis=0, keepdims=True)
     mid_s[2:3, :] = over
-    mid_s[3:4, :] = over
     for step in range(1, n_row):
         peer = lax.rem(row + step, n_row)
         copy = pltpu.make_async_remote_copy(
@@ -272,12 +287,12 @@
         growth = growth + got[1:2] + running * col_area
         running = running + got[0:1]
         over = over + got[2:3]
-    fin_s[0:1, :] = areas + factor * growth
-    fin_s[1:2, :] = areas
-    fin_s[2:3, :] = over
-    fin_s[3:4, :] = over
-    for step in col_steps:
-        peer = lax.rem(col + step, n_col)
+    line = lax.broadcasted_iota(jnp.int32, (8, LANES), 0)
+    sums = jnp.where(line == 0, areas + factor * growth, jnp.where(line == 1, areas, over))
+    sums = jnp.sum(sums, axis=1, keepdims=True)
+    lane = lax.broadcasted_iota(jnp.int32, (1, LANES), 1)
+    fin_s[...] = jnp.where(lane == 0, sums[0:1], jnp.where(lane == 1, sums[1:2], sums[2:3]))
+    for peer in peers:
         copy = pltpu.make_async_remote_copy(
             src_ref=fin_s, dst_ref=fin_r.at[col],
             send_sem=fin_ss.at[peer], recv_sem=fin_rs.at[col],
@@ -289,33 +304,36 @@
 
     inflation = 1.0 + factor * (within + carried)
     infl[...] = inflation
-    stores.append(pltpu.make_async_copy(infl, infl_h, out_sem.at[1]))
-    stores[1].start()
     i_hi, i_lo = split2(inflation.T)
     looked = dot(jnp.concatenate([i_hi, i_lo], axis=0), onehot[...])
     looked = looked[:tile_c] + looked[tile_c:]
     in_col = iota((tile_c, cells), 0) == jnp.broadcast_to(bin_col, (tile_c, cells))
     looked = jnp.sum(jnp.where(in_col, looked, 0.0), axis=0, keepdims=True)
-    grown = area[...] * looked
-
-    for step in reversed(col_steps):
-        peer = lax.rem(col + step, n_col)
+    grown[...] = area[...] * looked
+
+    for peer in reversed(peers):
         pltpu.make_async_remote_copy(
             src_ref=fin_s, dst_ref=fin_r.at[peer], send_sem=fin_ss.at[peer], recv_sem=fin_rs.at[peer],
             device_id={"col": peer}, device_id_type=MESH,
         ).wait_recv()
-    totals = fin_r[0]
-    for c in range(1, n_col):
-        totals = totals + fin_r[c]
-    totals = jnp.sum(totals, axis=1, keepdims=True)
-    sizes[...] = grown * (totals[1:2] / totals[0:1])
-    flag[...] = jnp.broadcast_to(totals[2:3], flag.shape)
-    stores.append(pltpu.make_async_copy(sizes, sizes_h, out_sem.at[2]))
-    stores.append(pltpu.make_async_copy(flag, flag_h, out_sem.at[3]))
-    for store in stores[2:]:
-        store.start()
+    parts = [fin_r[c] for c in range(n_col)]
+    while len(parts) > 1:
+        parts = [a + b for a, b in zip(parts[::2], parts[1::2])]
+    totals[...] = parts[0]
     for copy in started:
         copy.wait_send()
+
+
+def finish_kernel(rudy, infl, grown, totals, rudy_h, infl_h, sizes_h, sizes, sem):
+    stores = [
+        pltpu.make_async_copy(src, dst, sem.at[i])
+        for i, (src, dst) in enumerate(((rudy, rudy_h), (infl, infl_h), (sizes, sizes_h)))
+    ]
+    stores[0].start()
+    stores[1].start()
+    sums = totals[...]
+    sizes[...] = grown[...] * (sums[:, 1:2] / sums[:, 0:1])
+    stores[2].start()
     for store in stores:
         store.wait()
 
@@ -327,35 +345,46 @@
     vm = pltpu.VMEM
     dma = pltpu.SemaphoreType.DMA
     anywhere = pl.BlockSpec(memory_space=pl.ANY)
+    inside = pl.BlockSpec(memory_space=pltpu.VMEM)
     shape = jax.ShapeDtypeStruct
-    return pl.pallas_call(
+    held = pl.pallas_call(
         functools.partial(sparse_kernel, n_row, n_col),
         name="nets_to_tiles",
         out_shape=(
-            shape((tile_r, tile_c), F32), shape((tile_r, tile_c), F32),
-            shape((1, cells), F32), shape((1, LANES), F32),
+            vm((tile_r, tile_c), F32), vm((tile_r, tile_c), F32),
+            vm((1, cells), F32), vm((1, LANES), F32),
         ),
         in_specs=[anywhere] * 5,
-        out_specs=(anywhere,) * 4,
+        out_specs=(inside,) * 4,
         scratch_shapes=[
             vm((4, nets), jnp.int32), vm((1, nets), jnp.int32), vm((tile_r, tile_c), F32),
             vm((1, cells), jnp.int32), vm((1, cells), F32),
-            vm((tile_r, tile_c), F32), vm((tile_r, tile_c), F32), vm((1, cells), F32),
-            vm((1, LANES), F32),
             vm((16, nets), F32), vm((nets // LANES, LANES), F32),
-            vm((n_col, 8, LANES), F32), vm((n_col, 8, LANES), F32),
+            vm((n_col, ROWS, LANES), F32), vm((n_col, ROWS, LANES), F32),
             vm((tile_r, cells), BF16),
             vm((1, tile_c), F32), vm((n_row, 1, tile_c), F32),
-            vm((4, tile_c), F32), vm((n_row, 4, tile_c), F32),
-            vm((4, tile_c), F32), vm((n_col, 4, tile_c), F32),
-            dma((5,)), dma((4,)),
+            vm((3, tile_c), F32), vm((n_row, 3, tile_c), F32),
+            vm((1, tile_c), F32), vm((n_col, 1, tile_c), F32),
+            dma((5,)),
             dma((n_col,)), dma((n_col,)), dma((n_row,)), dma((n_row,)),
             dma((n_row,)), dma((n_row,)), dma((n_col,)), dma((n_col,)),
         ],
         compiler_params=pltpu.CompilerParams(
-            collective_id=0, has_side_effects=True, vmem_limit_bytes=40 * 1024 * 1024
+            collective_id=0, has_side_effects=True, vmem_limit_bytes=24 * 1024 * 1024
         ),
     )(boxes, pins.reshape(1, nets), capacity, cell_bin, cell_area)
+    outs = pl.pallas_call(
+        finish_kernel,
+        name="finish",
+        out_shape=(
+            shape((tile_r, tile_c), F32), shape((tile_r, tile_c), F32), shape((1, cells), F32),
+        ),
+        in_specs=[inside] * 4,
+        out_specs=(anywhere,) * 3,
+        scratch_shapes=[vm((1, cells), F32), dma((3,))],
+        compiler_params=pltpu.CompilerParams(vmem_limit_bytes=4 * 1024 * 1024),
+    )(*held)
+    return (*outs, held[3])
 
 
 def to_everyone(shard, axis):
@@ -405,14 +434,15 @@
 
 
 def per_device(n_row, n_col, *args):
-    rudy, inflation, cell_sizes, flag = sparse_program(n_row, n_col, *args)
+    rudy, inflation, cell_sizes, totals = sparse_program(n_row, n_col, *args)
+    flag = totals[0, 2]
 
     def again(state):
-        held = [jnp.where(state[3][0, 0] > 0.0, x, jnp.ones((), x.dtype)) for x in args]
+        held = [jnp.where(state[3] > 0.0, x, jnp.ones((), x.dtype)) for x in args]
         return (*dense_program(*held), jnp.zeros_like(flag))
 
     state = lax.while_loop(
-        lambda state: state[3][0, 0] > 0.0, again, (rudy, inflation, cell_sizes, flag)
+        lambda state: state[3] > 0.0, again, (rudy, inflation, cell_sizes, flag)
     )
     return state[:3]
 

time: 36.8 us -> 32.6 us (0.89)
  local copies, waits for them, and re-layouts: 4.63 us -> 0.59 us
    unnamed x3 -> x0, local copies, waits for them, and re-layouts: 4.63 us -> none
    pallas_call x1, Pallas kernels: 30.8 us -> 29.8 us  [sparse_program(): pl.pallas_call(functools.partial(sparse_kernel, n_row, n_col), name='nets...]
    pallas_call x0 -> x1, Pallas kernels: none -> 0.82 us  [sparse_program(): pl.pallas_call(finish_kernel, name='finish', out_shape=(shape((tile_r, ti...]
    slice x0 -> x1, local copies, waits for them, and re-layouts: none -> 0.59 us  [per_device(): flag = totals[0, 2]]
where the time goes in v2:
time: 32.6 us; the launch traced here: 32.5 us
  Pallas kernels  30.6 us (94%)
  between operations  0.65 us (2%)
  loops' own time  0.63 us (2%)
  local copies, waits for them, and re-layouts  0.59 us (2%)
    pallas_call x1, Pallas kernels, sparse_program(): pl.pallas_call(functools.partial(sparse_kernel, n_row, n_col), name='nets...  29.8 us
    pallas_call x1, Pallas kernels, sparse_program(): pl.pallas_call(finish_kernel, name='finish', out_shape=(shape((tile_r, ti...  0.82 us

profile of v2, /device:TPU:1, one launch (start us, length us, event | category | flops | bytes accessed | tf_op | source)
XLA Modules:
  0.0 32.5 jit_solution(10678985560863162600)
XLA Ops:
  0.6 29.8 %nets_to_tiles.1 = (f32[512,128]{1,0:T(8,128)S(1)}, f32[512,128]{1,0:T(8,128)S(1)}, f32[1,2048]{1,0:T(1,128)S(1)}, f32[1,128]{1,0:T(1,128)S(1)}) custom-call(s32[4,2048]{1,0:T(4,128)} %boxes_h.1, s32[1,2048]{1,0:T(1,128)} %bitcast.48, f32[512,128]{1,0:T(8,128)} %cap_h.1, s32[1,2048]{1,0:T(1,128)} %cbin_h.1, f32[1,2048]{1,0:T(1,128)} %area_h.1), custom_call_target="tpu_custom_call" | custom-call | tf_op jit(solution)/shard_map/nets_to_tiles/pallas_call | solution.py:350
  30.4 0.8 %finish.1 = (f32[512,128]{1,0:T(8,128)}, f32[512,128]{1,0:T(8,128)}, f32[1,2048]{1,0:T(1,128)}) custom-call(f32[512,128]{1,0:T(8,128)S(1)} %get-tuple-element.150.rudy, f32[512,128]{1,0:T(8,128)S(1)} %get-tuple-element.151.infl, f32[1,2048]{1,0:T(1,128)S(1)} %get-tuple-element.152.grown, f32[1,128]{1,0:T(1,128)S(1)} %get-tuple-element.153.totals), custom_call_target="tpu_custom_call" | custom-call | tf_op jit(solution)/shard_map/finish/pallas_call | solution.py:376
  31.3 0.6 %slice.27 = f32[1,1]{1,0:T(1,128)} slice(f32[1,128]{1,0:T(1,128)S(1)} %get-tuple-element.153.totals), slice={[0:1], [2:3]} | slice | bytes 8 | tf_op jit(solution)/shard_map/slice | solution.py:438
  31.8 0.6 %while.25 = (f32[512,128]{1,0:T(8,128)}, f32[512,128]{1,0:T(8,128)}, f32[1,2048]{1,0:T(1,128)}, f32[]{:T(128)}, s32[4,2048]{1,0:T(4,128)}, /*index=5*/s32[2048]{...) while((f32[512,128]{1,0:T(8,128)}, f32[512,128]{1,0:T(8,128)}, f32[1,2048]{1,0:T(1,128)}, f32[]{:T(128)}, ...), condition=%region_8.9_spmd, body=%region_0.8_spmd | while | flops 676364864 | bytes 11908902 | solution.py:444

commit v3 on v2

--- a/solution.py
+++ b/solution.py
@@ -42,8 +42,8 @@
     boxes_h, pins_h, cap_h, cbin_h, area_h,
     rudy, infl, grown, totals,
     boxes, pins, cap, cbin, area,
-    feat, hits, send, recv, onehot, early_s, early_r, mid_s, mid_r, fin_s, fin_r,
-    in_sem, a2a_ss, a2a_rs, early_ss, early_rs, mid_ss, mid_rs, fin_ss, fin_rs,
+    feat, hits, send, recv, onehot, early_s, early_r, mid_s, mid_r, fin_s, fin_r, fall,
+    in_sem, net_sent, net_got, early_sem, mid_sem, fin_sem,
 ):
     row = lax.axis_index("row")
     col = lax.axis_index("col")
@@ -62,6 +62,17 @@
     for load in loads:
         load.start()
 
+    def await_bytes(ref, count, sem):
+        some = ref.at[pl.ds(0, count)]
+        pltpu.make_async_copy(some, some, sem).wait()
+
+    def to_row(src, dst, sems):
+        for step in range(1, n_row):
+            pltpu.make_async_remote_copy(
+                src_ref=src, dst_ref=dst.at[row], send_sem=sems.at[0], recv_sem=sems.at[1],
+                device_id={"row": lax.rem(row + step, n_row)}, device_id_type=MESH,
+            ).start()
+
     barrier = pltpu.get_barrier_semaphore()
     chips = n_col // 2
     chip, core = col // 2, lax.rem(col, 2)
@@ -69,6 +80,11 @@
     peers = [2 * lax.rem(chip + o, chips) + k for o in far_first for k in range(2)]
     partner = 2 * chip + 1 - core
     peers.append(partner)
+    near_first = [0] + far_first[::-1]
+    cuts = [0, 5, 9, 13, 16] if chips == 16 else [0, chips]
+    groups = [near_first[a:b] for a, b in zip(cuts, cuts[1:])]
+    group_of = {o: g for g, group in enumerate(groups) for o in group}
+    steps = [o for o in far_first for k in range(2)] + [0]
     for peer in peers:
         pl.semaphore_signal(barrier, inc=1, device_id={"col": peer}, device_id_type=MESH)
     for step in range(1, n_row):
@@ -153,15 +169,12 @@
         send[d] = jnp.where(count_here, count[d : d + 1, :], block[0:8] + block[8:16])[0:ROWS]
 
     pl.semaphore_wait(barrier, n_col - 1 + n_row - 1)
-    started = []
-    for peer in peers:
-        copy = pltpu.make_async_remote_copy(
+    for peer, o in zip(peers, steps):
+        pltpu.make_async_remote_copy(
             src_ref=send.at[peer], dst_ref=recv.at[col],
-            send_sem=a2a_ss.at[peer], recv_sem=a2a_rs.at[col],
+            send_sem=net_sent, recv_sem=net_got.at[group_of[o]],
             device_id={"col": peer}, device_id_type=MESH,
-        )
-        copy.start()
-        started.append(copy)
+        ).start()
     recv[col] = send[col]
 
     loads[2].wait()
@@ -187,37 +200,20 @@
     bin_area = dot_nt(onehot[...], by_col)
     bin_area = bin_area[:, :tile_c] + bin_area[:, tile_c:]
     early_s[...] = jnp.sum(bin_area, axis=0, keepdims=True)
-    for step in range(1, n_row):
-        peer = lax.rem(row + step, n_row)
-        copy = pltpu.make_async_remote_copy(
-            src_ref=early_s, dst_ref=early_r.at[row],
-            send_sem=early_ss.at[peer], recv_sem=early_rs.at[row],
-            device_id={"row": peer}, device_id_type=MESH,
-        )
-        copy.start()
-        started.append(copy)
+    to_row(early_s, early_r, early_sem)
     early_r[row] = early_s[...]
-
-    def arrived(peer):
-        pltpu.make_async_remote_copy(
-            src_ref=send.at[peer], dst_ref=recv.at[peer],
-            send_sem=a2a_ss.at[peer], recv_sem=a2a_rs.at[peer],
-            device_id={"col": peer}, device_id_type=MESH,
-        ).wait_recv()
+    w_hi, w_lo = split2(bin_area)
+    upper = ones_where(iota((tile_r, tile_r), 0) <= iota((tile_r, tile_r), 1))
+    below = dot(upper, jnp.concatenate([w_hi, w_lo], axis=1))
+    fall[...] = below[:, :tile_c] + below[:, tile_c:]
 
     over = jnp.zeros((1, LANES), F32)
-    near_first = [0] + far_first[::-1]
-    cuts = [0, 6, 10, 14, 16] if chips == 16 else [0, chips]
     shift = (col * tile_c).astype(F32)
     lane = lax.broadcasted_iota(jnp.int32, (ROWS, LANES), 1)
-    for g in range(len(cuts) - 1):
+    for g, group in enumerate(groups):
         merged = []
-        for o in near_first[cuts[g] : cuts[g + 1]]:
-            if o == 0:
-                arrived(partner)
-            else:
-                arrived(2 * lax.rem(chip + o, chips))
-                arrived(2 * lax.rem(chip + o, chips) + 1)
+        await_bytes(recv, 2 * len(group) - (1 if g == 0 else 0), net_got.at[g])
+        for o in group:
             first = 2 * lax.rem(chip + o, chips)
             even, odds = recv[first], recv[first + 1]
             n_even, n_odd = even[4:5], odds[4:5]
@@ -247,38 +243,21 @@
 
     loads[4].wait()
     excess = jnp.maximum(rudy[...] - cap[...], 0.0)
+    mid_s[0:1, :] = jnp.sum(excess, axis=0, keepdims=True)
+    mid_s[1:2, :] = jnp.sum(excess * fall[...], axis=0, keepdims=True) + 1e30 * over
+    to_row(mid_s, mid_r, mid_sem)
+    mid_r[row] = mid_s[...]
     e_hi, e_lo = split2(excess)
     lower = ones_where(iota((tile_r, tile_r), 0) >= iota((tile_r, tile_r), 1))
     within = dot(lower, jnp.concatenate([e_hi, e_lo], axis=1))
-    within = within[:, :tile_c] + within[:, tile_c:]
-    mid_s[0:1, :] = within[tile_r - 1 : tile_r]
-    mid_s[1:2, :] = jnp.sum(bin_area * within, axis=0, keepdims=True)
-    mid_s[2:3, :] = over
-    for step in range(1, n_row):
-        peer = lax.rem(row + step, n_row)
-        copy = pltpu.make_async_remote_copy(
-            src_ref=mid_s, dst_ref=mid_r.at[row],
-            send_sem=mid_ss.at[peer], recv_sem=mid_rs.at[row],
-            device_id={"row": peer}, device_id_type=MESH,
-        )
-        copy.start()
-        started.append(copy)
-    mid_r[row] = mid_s[...]
-    for step in range(1, n_row):
-        peer = lax.rem(row + step, n_row)
-        for src, dst, ss, rs in (
-            (early_s, early_r, early_ss, early_rs), (mid_s, mid_r, mid_ss, mid_rs)
-        ):
-            pltpu.make_async_remote_copy(
-                src_ref=src, dst_ref=dst.at[peer], send_sem=ss.at[peer], recv_sem=rs.at[peer],
-                device_id={"row": peer}, device_id_type=MESH,
-            ).wait_recv()
+    infl[...] = within[:, :tile_c] + within[:, tile_c:]
+    await_bytes(early_r, n_row - 1, early_sem.at[1])
+    await_bytes(mid_r, n_row - 1, mid_sem.at[1])
     factor = 2.0 / (tile_r * n_row)
     running = jnp.zeros((1, tile_c), F32)
     carried = jnp.zeros((1, tile_c), F32)
     areas = jnp.zeros((1, tile_c), F32)
     growth = jnp.zeros((1, tile_c), F32)
-    over = jnp.zeros((1, tile_c), F32)
     for r in range(n_row):
         got = mid_r[r]
         col_area = early_r[r]
@@ -286,23 +265,16 @@
         areas = areas + col_area
         growth = growth + got[1:2] + running * col_area
         running = running + got[0:1]
-        over = over + got[2:3]
-    line = lax.broadcasted_iota(jnp.int32, (8, LANES), 0)
-    sums = jnp.where(line == 0, areas + factor * growth, jnp.where(line == 1, areas, over))
-    sums = jnp.sum(sums, axis=1, keepdims=True)
-    lane = lax.broadcasted_iota(jnp.int32, (1, LANES), 1)
-    fin_s[...] = jnp.where(lane == 0, sums[0:1], jnp.where(lane == 1, sums[1:2], sums[2:3]))
+    fin_s[0:1, :] = areas + factor * growth
+    fin_s[1:2, :] = areas
     for peer in peers:
-        copy = pltpu.make_async_remote_copy(
-            src_ref=fin_s, dst_ref=fin_r.at[col],
-            send_sem=fin_ss.at[peer], recv_sem=fin_rs.at[col],
+        pltpu.make_async_remote_copy(
+            src_ref=fin_s, dst_ref=fin_r.at[col], send_sem=fin_sem.at[0], recv_sem=fin_sem.at[1],
             device_id={"col": peer}, device_id_type=MESH,
-        )
-        copy.start()
-        started.append(copy)
+        ).start()
     fin_r[col] = fin_s[...]
 
-    inflation = 1.0 + factor * (within + carried)
+    inflation = 1.0 + factor * (infl[...] + carried)
     infl[...] = inflation
     i_hi, i_lo = split2(inflation.T)
     looked = dot(jnp.concatenate([i_hi, i_lo], axis=0), onehot[...])
@@ -311,28 +283,30 @@
     looked = jnp.sum(jnp.where(in_col, looked, 0.0), axis=0, keepdims=True)
     grown[...] = area[...] * looked
 
-    for peer in reversed(peers):
-        pltpu.make_async_remote_copy(
-            src_ref=fin_s, dst_ref=fin_r.at[peer], send_sem=fin_ss.at[peer], recv_sem=fin_rs.at[peer],
-            device_id={"col": peer}, device_id_type=MESH,
-        ).wait_recv()
+    await_bytes(send, n_col - 1, net_sent)
+    await_bytes(early_r, n_row - 1, early_sem.at[0])
+    await_bytes(mid_r, n_row - 1, mid_sem.at[0])
+    await_bytes(fin_r, n_col - 1, fin_sem.at[1])
     parts = [fin_r[c] for c in range(n_col)]
     while len(parts) > 1:
         parts = [a + b for a, b in zip(parts[::2], parts[1::2])]
     totals[...] = parts[0]
-    for copy in started:
-        copy.wait_send()
-
-
-def finish_kernel(rudy, infl, grown, totals, rudy_h, infl_h, sizes_h, sizes, sem):
+    await_bytes(fin_r, n_col - 1, fin_sem.at[0])
+
+
+def finish_kernel(rudy, infl, grown, totals, rudy_h, infl_h, sizes_h, flag_h, sizes, flag, sem):
     stores = [
         pltpu.make_async_copy(src, dst, sem.at[i])
-        for i, (src, dst) in enumerate(((rudy, rudy_h), (infl, infl_h), (sizes, sizes_h)))
+        for i, (src, dst) in enumerate(
+            ((rudy, rudy_h), (infl, infl_h), (sizes, sizes_h), (flag, flag_h))
+        )
     ]
     stores[0].start()
     stores[1].start()
-    sums = totals[...]
-    sizes[...] = grown[...] * (sums[:, 1:2] / sums[:, 0:1])
+    sums = jnp.sum(totals[...], axis=1, keepdims=True)
+    flag[...] = jnp.broadcast_to(sums[0:1], flag.shape)
+    stores[3].start()
+    sizes[...] = grown[...] * (sums[1:2] / sums[0:1])
     stores[2].start()
     for store in stores:
         store.wait()
@@ -352,7 +326,7 @@
         name="nets_to_tiles",
         out_shape=(
             vm((tile_r, tile_c), F32), vm((tile_r, tile_c), F32),
-            vm((1, cells), F32), vm((1, LANES), F32),
+            vm((1, cells), F32), vm((2, LANES), F32),
         ),
         in_specs=[anywhere] * 5,
         out_specs=(inside,) * 4,
@@ -363,28 +337,27 @@
             vm((n_col, ROWS, LANES), F32), vm((n_col, ROWS, LANES), F32),
             vm((tile_r, cells), BF16),
             vm((1, tile_c), F32), vm((n_row, 1, tile_c), F32),
-            vm((3, tile_c), F32), vm((n_row, 3, tile_c), F32),
-            vm((1, tile_c), F32), vm((n_col, 1, tile_c), F32),
-            dma((5,)),
-            dma((n_col,)), dma((n_col,)), dma((n_row,)), dma((n_row,)),
-            dma((n_row,)), dma((n_row,)), dma((n_col,)), dma((n_col,)),
+            vm((2, tile_c), F32), vm((n_row, 2, tile_c), F32),
+            vm((2, tile_c), F32), vm((n_col, 2, tile_c), F32),
+            vm((tile_r, tile_c), F32),
+            dma((5,)), dma(()), dma((4,)), dma((2,)), dma((2,)), dma((2,)),
         ],
         compiler_params=pltpu.CompilerParams(
             collective_id=0, has_side_effects=True, vmem_limit_bytes=24 * 1024 * 1024
         ),
     )(boxes, pins.reshape(1, nets), capacity, cell_bin, cell_area)
-    outs = pl.pallas_call(
+    return pl.pallas_call(
         finish_kernel,
         name="finish",
         out_shape=(
             shape((tile_r, tile_c), F32), shape((tile_r, tile_c), F32), shape((1, cells), F32),
+            shape((1, LANES), F32),
         ),
         in_specs=[inside] * 4,
-        out_specs=(anywhere,) * 3,
-        scratch_shapes=[vm((1, cells), F32), dma((3,))],
+        out_specs=(anywhere,) * 4,
+        scratch_shapes=[vm((1, cells), F32), vm((1, LANES), F32), dma((4,))],
         compiler_params=pltpu.CompilerParams(vmem_limit_bytes=4 * 1024 * 1024),
     )(*held)
-    return (*outs, held[3])
 
 
 def to_everyone(shard, axis):
@@ -434,15 +407,14 @@
 
 
 def per_device(n_row, n_col, *args):
-    rudy, inflation, cell_sizes, totals = sparse_program(n_row, n_col, *args)
-    flag = totals[0, 2]
+    rudy, inflation, cell_sizes, flag = sparse_program(n_row, n_col, *args)
 
     def again(state):
-        held = [jnp.where(state[3] > 0.0, x, jnp.ones((), x.dtype)) for x in args]
+        held = [jnp.where(state[3][0, 0] > 1e20, x, jnp.ones((), x.dtype)) for x in args]
         return (*dense_program(*held), jnp.zeros_like(flag))
 
     state = lax.while_loop(
-        lambda state: state[3] > 0.0, again, (rudy, inflation, cell_sizes, flag)
+        lambda state: state[3][0, 0] > 1e20, again, (rudy, inflation, cell_sizes, flag)
     )
     return state[:3]
 

time: 32.6 us -> 29.4 us (0.902)
  Pallas kernels: 30.6 us -> 28 us
  local copies, waits for them, and re-layouts: 0.59 us -> 0 us
    pallas_call x1, Pallas kernels: 29.8 us -> 27.2 us  [sparse_program(): pl.pallas_call(functools.partial(sparse_kernel, n_row, n_col), name='nets...]
    slice x1 -> x0, local copies, waits for them, and re-layouts: 0.59 us -> none  [per_device(): flag = totals[0, 2]]
where the time goes in v3:
time: 29.4 us; the launch traced here: 29.3 us
  Pallas kernels  28 us (95%)
  between operations  0.65 us (2%)
  loops' own time  0.62 us (2%)
    pallas_call x1, Pallas kernels, sparse_program(): pl.pallas_call(functools.partial(sparse_kernel, n_row, n_col), name='nets...  27.2 us
    pallas_call x1, Pallas kernels, sparse_program(): pl.pallas_call(finish_kernel, name='finish', out_shape=(shape((tile_r, ti...  0.83 us
    another operation x1, loops' own time, per_device(): lax.while_loop(lambda state: state[3][0, 0] > 1e+20, again, (rudy, inflat...  0.62 us

profile of v3, /device:TPU:1, one launch (start us, length us, event | category | flops | bytes accessed | tf_op | source)
XLA Modules:
  0.0 29.3 jit_solution(6785926496035775656)
XLA Ops:
  0.6 27.2 %nets_to_tiles.1 = (f32[512,128]{1,0:T(8,128)S(1)}, f32[512,128]{1,0:T(8,128)S(1)}, f32[1,2048]{1,0:T(1,128)S(1)}, f32[2,128]{1,0:T(2,128)S(1)}) custom-call(s32[4,2048]{1,0:T(4,128)} %boxes_h.1, s32[1,2048]{1,0:T(1,128)} %bitcast.83, f32[512,128]{1,0:T(8,128)} %cap_h.1, s32[1,2048]{1,0:T(1,128)} %cbin_h.1, f32[1,2048]{1,0:T(1,128)} %area_h.1), custom_call_target="tpu_custom_call" | custom-call | tf_op jit(solution)/shard_map/nets_to_tiles/pallas_call | solution.py:324
  27.9 0.8 %finish.1 = (f32[512,128]{1,0:T(8,128)}, f32[512,128]{1,0:T(8,128)}, f32[1,2048]{1,0:T(1,128)}, f32[1,128]{1,0:T(1,128)}) custom-call(f32[512,128]{1,0:T(8,128)S(1)} %get-tuple-element.216.rudy, f32[512,128]{1,0:T(8,128)S(1)} %get-tuple-element.217.infl, f32[1,2048]{1,0:T(1,128)S(1)} %get-tuple-element.218.grown, f32[2,128]{1,0:T(2,128)S(1)} %get-tuple-element.219.totals), custom_call_target="tpu_custom_call" | custom-call | tf_op jit(solution)/shard_map/finish/pallas_call | solution.py:349
  28.7 0.6 %while.36 = (f32[512,128]{1,0:T(8,128)}, f32[512,128]{1,0:T(8,128)}, f32[1,2048]{1,0:T(1,128)}, f32[1,128]{1,0:T(1,128)}, s32[4,2048]{1,0:T(4,128)}, /*index=5*/...) while((f32[512,128]{1,0:T(8,128)}, ...), condition=%wide.region_8.9_spmd, body=%wide.region_0.8_spmd.sunk | while | flops 676364864 | bytes 11909514 | solution.py:416

commit v4 on v3

--- a/solution.py
+++ b/solution.py
@@ -12,6 +12,7 @@
 BF16 = jnp.bfloat16
 SLOTS = 80
 ROWS = 5
+PIECES = 4
 HALF_SLOTS = 256
 LANES = 128
 
@@ -42,7 +43,7 @@
     boxes_h, pins_h, cap_h, cbin_h, area_h,
     rudy, infl, grown, totals,
     boxes, pins, cap, cbin, area,
-    feat, hits, send, recv, onehot, early_s, early_r, mid_s, mid_r, fin_s, fin_r, fall,
+    feat, hits, send, recv, onehot, early_s, early_r, mid_s, mid_r, fin_s, fin_r, fall, kept,
     in_sem, net_sent, net_got, early_sem, mid_sem, fin_sem,
 ):
     row = lax.axis_index("row")
@@ -66,11 +67,20 @@
         some = ref.at[pl.ds(0, count)]
         pltpu.make_async_copy(some, some, sem).wait()
 
-    def to_row(src, dst, sems):
-        for step in range(1, n_row):
+    quad, place4 = col // 4, lax.rem(col, 4)
+    member = row * 4 + place4
+    plane = [
+        (dr, {"row": lax.rem(row + dr, n_row), "col": 4 * quad + lax.rem(place4 + dq, 4)})
+        for dr in sorted(range(n_row), key=lambda d: -min(d, n_row - d) - 2 * (d % 2))
+        for dq in range(4)
+        if dr or dq
+    ]
+
+    def to_plane(src, dst, sems):
+        for _, peer in plane:
             pltpu.make_async_remote_copy(
-                src_ref=src, dst_ref=dst.at[row], send_sem=sems.at[0], recv_sem=sems.at[1],
-                device_id={"row": lax.rem(row + step, n_row)}, device_id_type=MESH,
+                src_ref=src, dst_ref=dst.at[member], send_sem=sems.at[0], recv_sem=sems.at[1],
+                device_id=peer, device_id_type=MESH,
             ).start()
 
     barrier = pltpu.get_barrier_semaphore()
@@ -87,10 +97,9 @@
     steps = [o for o in far_first for k in range(2)] + [0]
     for peer in peers:
         pl.semaphore_signal(barrier, inc=1, device_id={"col": peer}, device_id_type=MESH)
-    for step in range(1, n_row):
-        pl.semaphore_signal(
-            barrier, inc=1, device_id={"row": lax.rem(row + step, n_row)}, device_id_type=MESH
-        )
+    for dr, peer in plane:
+        if dr:
+            pl.semaphore_signal(barrier, inc=1, device_id=peer, device_id_type=MESH)
 
     loads[0].wait()
     loads[1].wait()
@@ -118,13 +127,13 @@
     for j in range(chunks):
         hits[j : j + 1, :] = in_band[:, j * LANES : (j + 1) * LANES]
     table = feat[...].astype(BF16)
-    member = hits[...].astype(BF16)
+    marks = hits[...].astype(BF16)
     ci, cj = iota((chunks, chunks), 0), iota((chunks, chunks), 1)
     per_half = chunks // 2
     same_half = jnp.where(ci >= per_half, 1.0, 0.0) == jnp.where(cj >= per_half, 1.0, 0.0)
-    ahead = dot(ones_where((ci > cj) & same_half), member)
+    ahead = dot(ones_where((ci > cj) & same_half), marks)
     before = ones_where(iota((LANES, LANES), 0) < iota((LANES, LANES), 1))
-    place = dot(member, before) + dot(ahead.astype(BF16), jnp.ones((LANES, LANES), BF16))
+    place = dot(marks, before) + dot(ahead.astype(BF16), jnp.ones((LANES, LANES), BF16))
     longest = jnp.max(place + hits[...], keepdims=True)
     place = jnp.where((hits[...] > 0.0) & (place < HALF_SLOTS), place, -1.0).astype(BF16)
     slot = iota((HALF_SLOTS, LANES), 0, BF16)
@@ -168,7 +177,7 @@
         block = jnp.concatenate([taken[d * SLOTS : (d + 1) * SLOTS], pad], axis=0).T
         send[d] = jnp.where(count_here, count[d : d + 1, :], block[0:8] + block[8:16])[0:ROWS]
 
-    pl.semaphore_wait(barrier, n_col - 1 + n_row - 1)
+    pl.semaphore_wait(barrier, n_col - 1 + 4 * (n_row - 1))
     for peer, o in zip(peers, steps):
         pltpu.make_async_remote_copy(
             src_ref=send.at[peer], dst_ref=recv.at[col],
@@ -200,13 +209,25 @@
     bin_area = dot_nt(onehot[...], by_col)
     bin_area = bin_area[:, :tile_c] + bin_area[:, tile_c:]
     early_s[...] = jnp.sum(bin_area, axis=0, keepdims=True)
-    to_row(early_s, early_r, early_sem)
-    early_r[row] = early_s[...]
+    to_plane(early_s, early_r, early_sem)
+    early_r[member] = early_s[...]
     w_hi, w_lo = split2(bin_area)
     upper = ones_where(iota((tile_r, tile_r), 0) <= iota((tile_r, tile_r), 1))
     below = dot(upper, jnp.concatenate([w_hi, w_lo], axis=1))
     fall[...] = below[:, :tile_c] + below[:, tile_c:]
 
+    loads[4].wait()
+    await_bytes(early_r, 4 * n_row - 1, early_sem.at[1])
+    factor = 2.0 / (tile_r * n_row)
+    areas_below = jnp.zeros((1, tile_c), F32)
+    areas = jnp.zeros((1, tile_c), F32)
+    for r in range(n_row):
+        column = early_r[4 * r + place4]
+        areas_below = areas_below + jnp.where(r > row, column, 0.0)
+        for q in range(4):
+            areas = areas + early_r[4 * r + q]
+    kept[0:1, :] = areas_below
+    kept[1:2, :] = areas
     over = jnp.zeros((1, LANES), F32)
     shift = (col * tile_c).astype(F32)
     lane = lax.broadcasted_iota(jnp.int32, (ROWS, LANES), 1)
@@ -241,38 +262,34 @@
             rows = slice(h * 256, (h + 1) * 256)
             rudy[rows, :] = part if g == 0 else rudy[rows, :] + part
 
-    loads[4].wait()
     excess = jnp.maximum(rudy[...] - cap[...], 0.0)
-    mid_s[0:1, :] = jnp.sum(excess, axis=0, keepdims=True)
-    mid_s[1:2, :] = jnp.sum(excess * fall[...], axis=0, keepdims=True) + 1e30 * over
-    to_row(mid_s, mid_r, mid_sem)
-    mid_r[row] = mid_s[...]
+    column = jnp.sum(excess, axis=0, keepdims=True)
+    mid_s[0:1, :] = column
+    mid_s[1:2, :] = (
+        jnp.sum(excess * fall[...], axis=0, keepdims=True) + column * kept[0:1, :] + 1e30 * over
+    )
+    to_plane(mid_s, mid_r, mid_sem)
+    mid_r[member] = mid_s[...]
     e_hi, e_lo = split2(excess)
     lower = ones_where(iota((tile_r, tile_r), 0) >= iota((tile_r, tile_r), 1))
     within = dot(lower, jnp.concatenate([e_hi, e_lo], axis=1))
     infl[...] = within[:, :tile_c] + within[:, tile_c:]
-    await_bytes(early_r, n_row - 1, early_sem.at[1])
-    await_bytes(mid_r, n_row - 1, mid_sem.at[1])
-    factor = 2.0 / (tile_r * n_row)
-    running = jnp.zeros((1, tile_c), F32)
+    await_bytes(mid_r, 4 * n_row - 1, mid_sem.at[1])
+    parts = [mid_r[m] for m in range(4 * n_row)]
+    while len(parts) > 1:
+        parts = [a + b for a, b in zip(parts[::2], parts[1::2])]
+    fin_s[0:1, :] = kept[1:2, :] + factor * parts[0][1:2]
+    fin_s[1:2, :] = kept[1:2, :]
+    quads = n_col // 4
+    for dz in sorted(range(1, quads), key=lambda d: -min(d, quads - d)):
+        pltpu.make_async_remote_copy(
+            src_ref=fin_s, dst_ref=fin_r.at[quad], send_sem=fin_sem.at[0], recv_sem=fin_sem.at[1],
+            device_id={"col": 4 * lax.rem(quad + dz, quads) + place4}, device_id_type=MESH,
+        ).start()
+    fin_r[quad] = fin_s[...]
     carried = jnp.zeros((1, tile_c), F32)
-    areas = jnp.zeros((1, tile_c), F32)
-    growth = jnp.zeros((1, tile_c), F32)
     for r in range(n_row):
-        got = mid_r[r]
-        col_area = early_r[r]
-        carried = jnp.where(row == r, running, carried)
-        areas = areas + col_area
-        growth = growth + got[1:2] + running * col_area
-        running = running + got[0:1]
-    fin_s[0:1, :] = areas + factor * growth
-    fin_s[1:2, :] = areas
-    for peer in peers:
-        pltpu.make_async_remote_copy(
-            src_ref=fin_s, dst_ref=fin_r.at[col], send_sem=fin_sem.at[0], recv_sem=fin_sem.at[1],
-            device_id={"col": peer}, device_id_type=MESH,
-        ).start()
-    fin_r[col] = fin_s[...]
+        carried = carried + jnp.where(r < row, mid_r[4 * r + place4][0:1], 0.0)
 
     inflation = 1.0 + factor * (infl[...] + carried)
     infl[...] = inflation
@@ -284,25 +301,26 @@
     grown[...] = area[...] * looked
 
     await_bytes(send, n_col - 1, net_sent)
-    await_bytes(early_r, n_row - 1, early_sem.at[0])
-    await_bytes(mid_r, n_row - 1, mid_sem.at[0])
-    await_bytes(fin_r, n_col - 1, fin_sem.at[1])
-    parts = [fin_r[c] for c in range(n_col)]
+    await_bytes(early_r, 4 * n_row - 1, early_sem.at[0])
+    await_bytes(mid_r, 4 * n_row - 1, mid_sem.at[0])
+    await_bytes(fin_r, quads - 1, fin_sem.at[1])
+    parts = [fin_r[c] for c in range(quads)]
     while len(parts) > 1:
         parts = [a + b for a, b in zip(parts[::2], parts[1::2])]
     totals[...] = parts[0]
-    await_bytes(fin_r, n_col - 1, fin_sem.at[0])
+    await_bytes(fin_r, quads - 1, fin_sem.at[0])
 
 
 def finish_kernel(rudy, infl, grown, totals, rudy_h, infl_h, sizes_h, flag_h, sizes, flag, sem):
-    stores = [
-        pltpu.make_async_copy(src, dst, sem.at[i])
-        for i, (src, dst) in enumerate(
-            ((rudy, rudy_h), (infl, infl_h), (sizes, sizes_h), (flag, flag_h))
-        )
-    ]
-    stores[0].start()
-    stores[1].start()
+    rows = rudy.shape[0] // PIECES
+    stores = []
+    for src, dst, done in ((rudy, rudy_h, sem.at[0]), (infl, infl_h, sem.at[1])):
+        for i in range(PIECES):
+            piece = pl.ds(i * rows, rows)
+            pltpu.make_async_copy(src.at[piece], dst.at[piece], done).start()
+        stores.append(pltpu.make_async_copy(src, dst, done))
+    stores.append(pltpu.make_async_copy(sizes, sizes_h, sem.at[2]))
+    stores.append(pltpu.make_async_copy(flag, flag_h, sem.at[3]))
     sums = jnp.sum(totals[...], axis=1, keepdims=True)
     flag[...] = jnp.broadcast_to(sums[0:1], flag.shape)
     stores[3].start()
@@ -336,10 +354,10 @@
             vm((16, nets), F32), vm((nets // LANES, LANES), F32),
             vm((n_col, ROWS, LANES), F32), vm((n_col, ROWS, LANES), F32),
             vm((tile_r, cells), BF16),
-            vm((1, tile_c), F32), vm((n_row, 1, tile_c), F32),
-            vm((2, tile_c), F32), vm((n_row, 2, tile_c), F32),
-            vm((2, tile_c), F32), vm((n_col, 2, tile_c), F32),
-            vm((tile_r, tile_c), F32),
+            vm((1, tile_c), F32), vm((4 * n_row, 1, tile_c), F32),
+            vm((2, tile_c), F32), vm((4 * n_row, 2, tile_c), F32),
+            vm((2, tile_c), F32), vm((n_col // 4, 2, tile_c), F32),
+            vm((tile_r, tile_c), F32), vm((2, tile_c), F32),
             dma((5,)), dma(()), dma((4,)), dma((2,)), dma((2,)), dma((2,)),
         ],
         compiler_params=pltpu.CompilerParams(

time: 29.4 us -> 29.6 us (level)
  Pallas kernels: 28 us -> 28.3 us
where the time goes in v4:
time: 29.6 us; the launch traced here: 29.5 us
  Pallas kernels  28.3 us (96%)
  between operations  0.65 us (2%)
  loops' own time  0.62 us (2%)
    pallas_call x1, Pallas kernels, sparse_program(): pl.pallas_call(functools.partial(sparse_kernel, n_row, n_col), name='nets...  27.4 us
    pallas_call x1, Pallas kernels, sparse_program(): pl.pallas_call(finish_kernel, name='finish', out_shape=(shape((tile_r, ti...  0.84 us
    another operation x1, loops' own time, per_device(): lax.while_loop(lambda state: state[3][0, 0] > 1e+20, again, (rudy, inflat...  0.62 us

profile of v4, /device:TPU:1, one launch (start us, length us, event | category | flops | bytes accessed | tf_op | source)
XLA Modules:
  0.0 29.5 jit_solution(11948633148163842973)
XLA Ops:
  0.6 27.4 %nets_to_tiles.1 = (f32[512,128]{1,0:T(8,128)S(1)}, f32[512,128]{1,0:T(8,128)S(1)}, f32[1,2048]{1,0:T(1,128)S(1)}, f32[2,128]{1,0:T(2,128)S(1)}) custom-call(s32[4,2048]{1,0:T(4,128)} %boxes_h.1, s32[1,2048]{1,0:T(1,128)} %bitcast.83, f32[512,128]{1,0:T(8,128)} %cap_h.1, s32[1,2048]{1,0:T(1,128)} %cbin_h.1, f32[1,2048]{1,0:T(1,128)} %area_h.1), custom_call_target="tpu_custom_call" | custom-call | tf_op jit(solution)/shard_map/nets_to_tiles/pallas_call | solution.py:342
  28.1 0.8 %finish.1 = (f32[512,128]{1,0:T(8,128)}, f32[512,128]{1,0:T(8,128)}, f32[1,2048]{1,0:T(1,128)}, f32[1,128]{1,0:T(1,128)}) custom-call(f32[512,128]{1,0:T(8,128)S(1)} %get-tuple-element.216.rudy, f32[512,128]{1,0:T(8,128)S(1)} %get-tuple-element.217.infl, f32[1,2048]{1,0:T(1,128)S(1)} %get-tuple-element.218.grown, f32[2,128]{1,0:T(2,128)S(1)} %get-tuple-element.219.totals), custom_call_target="tpu_custom_call" | custom-call | tf_op jit(solution)/shard_map/finish/pallas_call | solution.py:367
  28.9 0.6 %while.36 = (f32[512,128]{1,0:T(8,128)}, f32[512,128]{1,0:T(8,128)}, f32[1,2048]{1,0:T(1,128)}, f32[1,128]{1,0:T(1,128)}, s32[4,2048]{1,0:T(4,128)}, /*index=5*/...) while((f32[512,128]{1,0:T(8,128)}, ...), condition=%wide.region_8.9_spmd, body=%wide.region_0.8_spmd.sunk | while | flops 676364864 | bytes 11909514 | solution.py:434

commit v5 on v4

--- a/solution.py
+++ b/solution.py
@@ -76,10 +76,16 @@
         if dr or dq
     ]
 
-    def to_plane(src, dst, sems):
-        for _, peer in plane:
+    row_peers = [
+        {"row": lax.rem(row + step, n_row)}
+        for step in sorted(range(1, n_row), key=lambda d: -min(d, n_row - d) - 2 * (d % 2))
+    ]
+    plane = [peer for _, peer in plane]
+
+    def push(src, dst, sems, targets):
+        for peer in targets:
             pltpu.make_async_remote_copy(
-                src_ref=src, dst_ref=dst.at[member], send_sem=sems.at[0], recv_sem=sems.at[1],
+                src_ref=src, dst_ref=dst, send_sem=sems.at[0], recv_sem=sems.at[1],
                 device_id=peer, device_id_type=MESH,
             ).start()
 
@@ -97,9 +103,8 @@
     steps = [o for o in far_first for k in range(2)] + [0]
     for peer in peers:
         pl.semaphore_signal(barrier, inc=1, device_id={"col": peer}, device_id_type=MESH)
-    for dr, peer in plane:
-        if dr:
-            pl.semaphore_signal(barrier, inc=1, device_id=peer, device_id_type=MESH)
+    for peer in row_peers:
+        pl.semaphore_signal(barrier, inc=1, device_id=peer, device_id_type=MESH)
 
     loads[0].wait()
     loads[1].wait()
@@ -177,7 +182,7 @@
         block = jnp.concatenate([taken[d * SLOTS : (d + 1) * SLOTS], pad], axis=0).T
         send[d] = jnp.where(count_here, count[d : d + 1, :], block[0:8] + block[8:16])[0:ROWS]
 
-    pl.semaphore_wait(barrier, n_col - 1 + 4 * (n_row - 1))
+    pl.semaphore_wait(barrier, n_col - 1 + n_row - 1)
     for peer, o in zip(peers, steps):
         pltpu.make_async_remote_copy(
             src_ref=send.at[peer], dst_ref=recv.at[col],
@@ -209,30 +214,25 @@
     bin_area = dot_nt(onehot[...], by_col)
     bin_area = bin_area[:, :tile_c] + bin_area[:, tile_c:]
     early_s[...] = jnp.sum(bin_area, axis=0, keepdims=True)
-    to_plane(early_s, early_r, early_sem)
-    early_r[member] = early_s[...]
+    push(early_s, early_r.at[row], early_sem, row_peers)
+    early_r[row] = early_s[...]
     w_hi, w_lo = split2(bin_area)
     upper = ones_where(iota((tile_r, tile_r), 0) <= iota((tile_r, tile_r), 1))
     below = dot(upper, jnp.concatenate([w_hi, w_lo], axis=1))
     fall[...] = below[:, :tile_c] + below[:, tile_c:]
 
     loads[4].wait()
-    await_bytes(early_r, 4 * n_row - 1, early_sem.at[1])
-    factor = 2.0 / (tile_r * n_row)
-    areas_below = jnp.zeros((1, tile_c), F32)
-    areas = jnp.zeros((1, tile_c), F32)
-    for r in range(n_row):
-        column = early_r[4 * r + place4]
-        areas_below = areas_below + jnp.where(r > row, column, 0.0)
-        for q in range(4):
-            areas = areas + early_r[4 * r + q]
-    kept[0:1, :] = areas_below
-    kept[1:2, :] = areas
     over = jnp.zeros((1, LANES), F32)
     shift = (col * tile_c).astype(F32)
     lane = lax.broadcasted_iota(jnp.int32, (ROWS, LANES), 1)
     for g, group in enumerate(groups):
         merged = []
+        if g == len(groups) - 1:
+            await_bytes(early_r, n_row - 1, early_sem.at[1])
+            areas_below = jnp.zeros((1, tile_c), F32)
+            for r in range(n_row):
+                areas_below = areas_below + jnp.where(r > row, early_r[r], 0.0)
+            kept[...] = areas_below
         await_bytes(recv, 2 * len(group) - (1 if g == 0 else 0), net_got.at[g])
         for o in group:
             first = 2 * lax.rem(chip + o, chips)
@@ -266,9 +266,10 @@
     column = jnp.sum(excess, axis=0, keepdims=True)
     mid_s[0:1, :] = column
     mid_s[1:2, :] = (
-        jnp.sum(excess * fall[...], axis=0, keepdims=True) + column * kept[0:1, :] + 1e30 * over
-    )
-    to_plane(mid_s, mid_r, mid_sem)
+        jnp.sum(excess * fall[...], axis=0, keepdims=True) + column * kept[...] + 1e30 * over
+    )
+    mid_s[2:3, :] = early_s[...]
+    push(mid_s, mid_r.at[member], mid_sem, plane)
     mid_r[member] = mid_s[...]
     e_hi, e_lo = split2(excess)
     lower = ones_where(iota((tile_r, tile_r), 0) >= iota((tile_r, tile_r), 1))
@@ -278,14 +279,17 @@
     parts = [mid_r[m] for m in range(4 * n_row)]
     while len(parts) > 1:
         parts = [a + b for a, b in zip(parts[::2], parts[1::2])]
-    fin_s[0:1, :] = kept[1:2, :] + factor * parts[0][1:2]
-    fin_s[1:2, :] = kept[1:2, :]
+    factor = 2.0 / (tile_r * n_row)
+    fin_s[0:1, :] = parts[0][2:3] + factor * parts[0][1:2]
+    fin_s[1:2, :] = parts[0][2:3]
     quads = n_col // 4
-    for dz in sorted(range(1, quads), key=lambda d: -min(d, quads - d)):
-        pltpu.make_async_remote_copy(
-            src_ref=fin_s, dst_ref=fin_r.at[quad], send_sem=fin_sem.at[0], recv_sem=fin_sem.at[1],
-            device_id={"col": 4 * lax.rem(quad + dz, quads) + place4}, device_id_type=MESH,
-        ).start()
+    push(
+        fin_s, fin_r.at[quad], fin_sem,
+        [
+            {"col": 4 * lax.rem(quad + dz, quads) + place4}
+            for dz in sorted(range(1, quads), key=lambda d: -min(d, quads - d))
+        ],
+    )
     fin_r[quad] = fin_s[...]
     carried = jnp.zeros((1, tile_c), F32)
     for r in range(n_row):
@@ -301,7 +305,7 @@
     grown[...] = area[...] * looked
 
     await_bytes(send, n_col - 1, net_sent)
-    await_bytes(early_r, 4 * n_row - 1, early_sem.at[0])
+    await_bytes(early_r, n_row - 1, early_sem.at[0])
     await_bytes(mid_r, 4 * n_row - 1, mid_sem.at[0])
     await_bytes(fin_r, quads - 1, fin_sem.at[1])
     parts = [fin_r[c] for c in range(quads)]
@@ -354,10 +358,10 @@
             vm((16, nets), F32), vm((nets // LANES, LANES), F32),
             vm((n_col, ROWS, LANES), F32), vm((n_col, ROWS, LANES), F32),
             vm((tile_r, cells), BF16),
-            vm((1, tile_c), F32), vm((4 * n_row, 1, tile_c), F32),
-            vm((2, tile_c), F32), vm((4 * n_row, 2, tile_c), F32),
+            vm((1, tile_c), F32), vm((n_row, 1, tile_c), F32),
+            vm((3, tile_c), F32), vm((4 * n_row, 3, tile_c), F32),
             vm((2, tile_c), F32), vm((n_col // 4, 2, tile_c), F32),
-            vm((tile_r, tile_c), F32), vm((2, tile_c), F32),
+            vm((tile_r, tile_c), F32), vm((1, tile_c), F32),
             dma((5,)), dma(()), dma((4,)), dma((2,)), dma((2,)), dma((2,)),
         ],
         compiler_params=pltpu.CompilerParams(

time: 29.6 us -> 28.6 us (0.966)
  Pallas kernels: 28.3 us -> 27.2 us
    pallas_call x1, Pallas kernels: 27.4 us -> 26.3 us  [sparse_program(): pl.pallas_call(functools.partial(sparse_kernel, n_row, n_col), name='nets...]
where the time goes in v5:
time: 28.6 us; the launch traced here: 28.4 us
  Pallas kernels  27.2 us (95%)
  between operations  0.65 us (2%)
  loops' own time  0.62 us (2%)
    pallas_call x1, Pallas kernels, sparse_program(): pl.pallas_call(functools.partial(sparse_kernel, n_row, n_col), name='nets...  26.3 us
    pallas_call x1, Pallas kernels, sparse_program(): pl.pallas_call(finish_kernel, name='finish', out_shape=(shape((tile_r, ti...  0.84 us
    another operation x1, loops' own time, per_device(): lax.while_loop(lambda state: state[3][0, 0] > 1e+20, again, (rudy, inflat...  0.62 us

profile of v5, /device:TPU:1, one launch (start us, length us, event | category | flops | bytes accessed | tf_op | source)
XLA Modules:
  0.0 28.4 jit_solution(9810592859120616604)
XLA Ops:
  0.6 26.3 %nets_to_tiles.1 = (f32[512,128]{1,0:T(8,128)S(1)}, f32[512,128]{1,0:T(8,128)S(1)}, f32[1,2048]{1,0:T(1,128)S(1)}, f32[2,128]{1,0:T(2,128)S(1)}) custom-call(s32[4,2048]{1,0:T(4,128)} %boxes_h.1, s32[1,2048]{1,0:T(1,128)} %bitcast.83, f32[512,128]{1,0:T(8,128)} %cap_h.1, s32[1,2048]{1,0:T(1,128)} %cbin_h.1, f32[1,2048]{1,0:T(1,128)} %area_h.1), custom_call_target="tpu_custom_call" | custom-call | tf_op jit(solution)/shard_map/nets_to_tiles/pallas_call | solution.py:346
  27.0 0.8 %finish.1 = (f32[512,128]{1,0:T(8,128)}, f32[512,128]{1,0:T(8,128)}, f32[1,2048]{1,0:T(1,128)}, f32[1,128]{1,0:T(1,128)}) custom-call(f32[512,128]{1,0:T(8,128)S(1)} %get-tuple-element.216.rudy, f32[512,128]{1,0:T(8,128)S(1)} %get-tuple-element.217.infl, f32[1,2048]{1,0:T(1,128)S(1)} %get-tuple-element.218.grown, f32[2,128]{1,0:T(2,128)S(1)} %get-tuple-element.219.totals), custom_call_target="tpu_custom_call" | custom-call | tf_op jit(solution)/shard_map/finish/pallas_call | solution.py:371
  27.8 0.6 %while.36 = (f32[512,128]{1,0:T(8,128)}, f32[512,128]{1,0:T(8,128)}, f32[1,2048]{1,0:T(1,128)}, f32[1,128]{1,0:T(1,128)}, s32[4,2048]{1,0:T(4,128)}, /*index=5*/...) while((f32[512,128]{1,0:T(8,128)}, ...), condition=%wide.region_8.9_spmd, body=%wide.region_0.8_spmd.sunk | while | flops 676364864 | bytes 11909514 | solution.py:438

commit v6 on v5

--- a/solution.py
+++ b/solution.py
@@ -43,8 +43,8 @@
     boxes_h, pins_h, cap_h, cbin_h, area_h,
     rudy, infl, grown, totals,
     boxes, pins, cap, cbin, area,
-    feat, hits, send, recv, onehot, early_s, early_r, mid_s, mid_r, fin_s, fin_r, fall, kept,
-    in_sem, net_sent, net_got, early_sem, mid_sem, fin_sem,
+    feat, hits, ahead_or_all, lists, swapped, send, recv, spill, onehot, early_s, early_r, mid_s, mid_r, fin_s, fin_r, fall, kept,
+    in_sem, swap_sem, net_sent, net_got, early_sem, mid_sem, fin_sem,
 ):
     row = lax.axis_index("row")
     col = lax.axis_index("col")
@@ -70,17 +70,17 @@
     quad, place4 = col // 4, lax.rem(col, 4)
     member = row * 4 + place4
     plane = [
-        (dr, {"row": lax.rem(row + dr, n_row), "col": 4 * quad + lax.rem(place4 + dq, 4)})
-        for dr in sorted(range(n_row), key=lambda d: -min(d, n_row - d) - 2 * (d % 2))
-        for dq in range(4)
-        if dr or dq
+        {"row": lax.rem(row + dr, n_row), "col": 4 * quad + lax.rem(place4 + dq, 4)}
+        for dr, dq in sorted(
+            [(dr, dq) for dr in range(n_row) for dq in range(4) if dr or dq],
+            key=lambda d: -min(d[0], n_row - d[0]) / 2 - 2 * (d[0] % 2) - 1.5 * (d[1] % 2),
+        )
     ]
 
     row_peers = [
         {"row": lax.rem(row + step, n_row)}
         for step in sorted(range(1, n_row), key=lambda d: -min(d, n_row - d) - 2 * (d % 2))
     ]
-    plane = [peer for _, peer in plane]
 
     def push(src, dst, sems, targets):
         for peer in targets:
@@ -93,18 +93,24 @@
     chips = n_col // 2
     chip, core = col // 2, lax.rem(col, 2)
     far_first = sorted(range(1, chips), key=lambda o: -min(o, chips - o))
-    peers = [2 * lax.rem(chip + o, chips) + k for o in far_first for k in range(2)]
-    partner = 2 * chip + 1 - core
-    peers.append(partner)
+    chip_peers = [(o, lax.rem(chip + o, chips)) for o in far_first]
+    partner = {"col": 2 * chip + 1 - core}
+    for _, peer in chip_peers:
+        pl.semaphore_signal(
+            barrier, inc=1, device_id={"col": 2 * peer + core}, device_id_type=MESH
+        )
+    pl.semaphore_signal(barrier, inc=1, device_id=partner, device_id_type=MESH)
     near_first = [0] + far_first[::-1]
     cuts = [0, 5, 9, 13, 16] if chips == 16 else [0, chips]
     groups = [near_first[a:b] for a, b in zip(cuts, cuts[1:])]
     group_of = {o: g for g, group in enumerate(groups) for o in group}
-    steps = [o for o in far_first for k in range(2)] + [0]
-    for peer in peers:
-        pl.semaphore_signal(barrier, inc=1, device_id={"col": peer}, device_id_type=MESH)
     for peer in row_peers:
         pl.semaphore_signal(barrier, inc=1, device_id=peer, device_id_type=MESH)
+
+    band_slots = 2 * HALF_SLOTS
+    wide = band_slots + LANES
+    ti, tj = iota((band_slots, wide), 0), iota((band_slots, wide), 1)
+    ahead_or_all[...] = jnp.where(tj >= band_slots, 1.0, jnp.where(ti < tj, 1.0, 0.0)).astype(BF16)
 
     loads[0].wait()
     loads[1].wait()
@@ -154,42 +160,43 @@
         packed.append(dot_nt(pick, table[:, h * half : (h + 1) * half]).T)
     packed = jnp.concatenate(packed, axis=1)
     listed = packed[0:8] + packed[8:16]
-    band_slots = 2 * HALF_SLOTS
 
     tile_x = iota((n_col, band_slots), 0) * tile_c
     meets = (listed[0:1] < tile_x + tile_c) & (listed[1:2] > tile_x)
-    wide = band_slots + LANES
-    ti, tj = iota((band_slots, wide), 0), iota((band_slots, wide), 1)
-    counted = dot(ones_where(meets), ones_where((ti < tj) | (tj >= band_slots)))
+    counted = dot(ones_where(meets), ahead_or_all[...])
     order = counted[:, :band_slots]
     count = jnp.where(longest > HALF_SLOTS, 1e6, counted[:, band_slots:])
     odd = core.astype(F32)
     order = jnp.where(meets, odd * (SLOTS - 1) + (1.0 - 2.0 * odd) * order, -1.0).astype(BF16)
     slot = iota((SLOTS, band_slots), 0, BF16)
-    pick = jnp.concatenate(
-        [
-            ones_where(slot == jnp.broadcast_to(order[d : d + 1, :], slot.shape))
-            for d in range(n_col)
-        ],
-        axis=0,
-    )
-    taken = dot_nt(pick, packed.astype(BF16))
-    pad = jnp.zeros((LANES - SLOTS, 16), F32)
+    share = min(8, chips)
+    packed = jnp.concatenate([packed.astype(BF16)] * share, axis=0)
+    pad = jnp.zeros((LANES - SLOTS, 16 * share), F32)
+    lane16 = lax.broadcasted_iota(jnp.int32, (SLOTS, 16 * share), 1)
     line = lax.broadcasted_iota(jnp.int32, (8, LANES), 0)
-    lane8 = lax.broadcasted_iota(jnp.int32, (8, LANES), 1)
-    count_here = (line == 4) & (lane8 >= SLOTS)
-    for d in range(n_col):
-        block = jnp.concatenate([taken[d * SLOTS : (d + 1) * SLOTS], pad], axis=0).T
-        send[d] = jnp.where(count_here, count[d : d + 1, :], block[0:8] + block[8:16])[0:ROWS]
-
-    pl.semaphore_wait(barrier, n_col - 1 + n_row - 1)
-    for peer, o in zip(peers, steps):
-        pltpu.make_async_remote_copy(
-            src_ref=send.at[peer], dst_ref=recv.at[col],
-            send_sem=net_sent, recv_sem=net_got.at[group_of[o]],
-            device_id={"col": peer}, device_id_type=MESH,
-        ).start()
-    recv[col] = send[col]
+    taken = []
+    for parity in range(2):
+        pick = jnp.concatenate(
+            [
+                ones_where(slot == jnp.broadcast_to(order[d : d + 1, :], slot.shape))
+                for d in range(parity, n_col, 2)
+            ],
+            axis=0,
+        )
+        taken.append(dot_nt(pick, packed))
+    for first in range(0, chips, share):
+        for parity in range(2):
+            mixed = taken[parity][first * SLOTS : (first + 1) * SLOTS]
+            for j in range(1, share):
+                rows = slice((first + j) * SLOTS, (first + j + 1) * SLOTS)
+                mixed = jnp.where(lane16 >= 16 * j, taken[parity][rows], mixed)
+            turned = jnp.concatenate([mixed, pad], axis=0).T
+            for j in range(share):
+                d = 2 * (first + j) + parity
+                block = turned[16 * j : 16 * j + 8] + turned[16 * j + 8 : 16 * j + 16]
+                block = pltpu.roll(block, core * (LANES - SLOTS), 1)
+                block = jnp.where(line == ROWS, count[d : d + 1, :], block)
+                lists[parity, first + j] = block[0 : ROWS + 1]
 
     loads[2].wait()
     loads[3].wait()
@@ -214,35 +221,49 @@
     bin_area = dot_nt(onehot[...], by_col)
     bin_area = bin_area[:, :tile_c] + bin_area[:, tile_c:]
     early_s[...] = jnp.sum(bin_area, axis=0, keepdims=True)
+
+    pl.semaphore_wait(barrier, chips + n_row - 1)
+    swap = pltpu.make_async_remote_copy(
+        src_ref=lists.at[1 - core], dst_ref=swapped, send_sem=swap_sem.at[0],
+        recv_sem=swap_sem.at[1], device_id=partner, device_id_type=MESH,
+    )
+    swap.start()
     push(early_s, early_r.at[row], early_sem, row_peers)
     early_r[row] = early_s[...]
+    swap.wait_recv()
+    for p in range(chips):
+        send[p] = (lists[core, p] + swapped[p])[0:ROWS]
+    for o, peer in chip_peers:
+        pltpu.make_async_remote_copy(
+            src_ref=send.at[peer], dst_ref=recv.at[chip],
+            send_sem=net_sent, recv_sem=net_got.at[group_of[o]],
+            device_id={"col": 2 * peer + core}, device_id_type=MESH,
+        ).start()
+    recv[chip] = send[chip]
+    over = jnp.zeros((1, LANES), F32)
+    for p in range(chips):
+        ours, theirs = lists[core, p][ROWS:], swapped[p][ROWS:]
+        spilt = (ours > SLOTS) | (theirs > SLOTS) | (ours + theirs > LANES)
+        over = over + jnp.where(spilt, 1.0, 0.0)
+    spill[...] = over
+
+    await_bytes(early_r, n_row - 1, early_sem.at[0])
     w_hi, w_lo = split2(bin_area)
     upper = ones_where(iota((tile_r, tile_r), 0) <= iota((tile_r, tile_r), 1))
     below = dot(upper, jnp.concatenate([w_hi, w_lo], axis=1))
     fall[...] = below[:, :tile_c] + below[:, tile_c:]
 
     loads[4].wait()
-    over = jnp.zeros((1, LANES), F32)
     shift = (col * tile_c).astype(F32)
-    lane = lax.broadcasted_iota(jnp.int32, (ROWS, LANES), 1)
     for g, group in enumerate(groups):
-        merged = []
         if g == len(groups) - 1:
             await_bytes(early_r, n_row - 1, early_sem.at[1])
             areas_below = jnp.zeros((1, tile_c), F32)
             for r in range(n_row):
                 areas_below = areas_below + jnp.where(r > row, early_r[r], 0.0)
             kept[...] = areas_below
-        await_bytes(recv, 2 * len(group) - (1 if g == 0 else 0), net_got.at[g])
-        for o in group:
-            first = 2 * lax.rem(chip + o, chips)
-            even, odds = recv[first], recv[first + 1]
-            n_even, n_odd = even[4:5], odds[4:5]
-            spilt = (n_even > SLOTS) | (n_odd > SLOTS) | (n_even + n_odd > LANES)
-            over = over + jnp.where(spilt & (lane[0:1] >= SLOTS), 1.0, 0.0)
-            even = jnp.where(lane < SLOTS, even, 0.0)
-            odds = jnp.where(lane < SLOTS, odds, 0.0)
-            merged.append(even + pltpu.roll(odds, LANES - SLOTS, 1))
+        await_bytes(recv, len(group) - (1 if g == 0 else 0), net_got.at[g])
+        merged = [recv[lax.rem(chip + o, chips)] for o in group]
         merged = jnp.concatenate(merged, axis=1)
         total = merged.shape[1]
         full = lambda x, n: jnp.broadcast_to(x, (n, total))
@@ -266,12 +287,14 @@
     column = jnp.sum(excess, axis=0, keepdims=True)
     mid_s[0:1, :] = column
     mid_s[1:2, :] = (
-        jnp.sum(excess * fall[...], axis=0, keepdims=True) + column * kept[...] + 1e30 * over
+        jnp.sum(excess * fall[...], axis=0, keepdims=True) + column * kept[...]
+        + 1e30 * spill[...]
     )
     mid_s[2:3, :] = early_s[...]
     push(mid_s, mid_r.at[member], mid_sem, plane)
     mid_r[member] = mid_s[...]
-    e_hi, e_lo = split2(excess)
+    swap.wait_send()
+    e_hi, e_lo = split2(jnp.maximum(rudy[...] - cap[...], 0.0))
     lower = ones_where(iota((tile_r, tile_r), 0) >= iota((tile_r, tile_r), 1))
     within = dot(lower, jnp.concatenate([e_hi, e_lo], axis=1))
     infl[...] = within[:, :tile_c] + within[:, tile_c:]
@@ -304,8 +327,7 @@
     looked = jnp.sum(jnp.where(in_col, looked, 0.0), axis=0, keepdims=True)
     grown[...] = area[...] * looked
 
-    await_bytes(send, n_col - 1, net_sent)
-    await_bytes(early_r, n_row - 1, early_sem.at[0])
+    await_bytes(send, chips - 1, net_sent)
     await_bytes(mid_r, 4 * n_row - 1, mid_sem.at[0])
     await_bytes(fin_r, quads - 1, fin_sem.at[1])
     parts = [fin_r[c] for c in range(quads)]
@@ -356,13 +378,16 @@
             vm((4, nets), jnp.int32), vm((1, nets), jnp.int32), vm((tile_r, tile_c), F32),
             vm((1, cells), jnp.int32), vm((1, cells), F32),
             vm((16, nets), F32), vm((nets // LANES, LANES), F32),
-            vm((n_col, ROWS, LANES), F32), vm((n_col, ROWS, LANES), F32),
+            vm((2 * HALF_SLOTS, 2 * HALF_SLOTS + LANES), BF16),
+            vm((2, n_col // 2, ROWS + 1, LANES), F32), vm((n_col // 2, ROWS + 1, LANES), F32),
+            vm((n_col // 2, ROWS, LANES), F32), vm((n_col // 2, ROWS, LANES), F32),
+            vm((1, LANES), F32),
             vm((tile_r, cells), BF16),
             vm((1, tile_c), F32), vm((n_row, 1, tile_c), F32),
             vm((3, tile_c), F32), vm((4 * n_row, 3, tile_c), F32),
             vm((2, tile_c), F32), vm((n_col // 4, 2, tile_c), F32),
             vm((tile_r, tile_c), F32), vm((1, tile_c), F32),
-            dma((5,)), dma(()), dma((4,)), dma((2,)), dma((2,)), dma((2,)),
+            dma((5,)), dma((2,)), dma(()), dma((4,)), dma((2,)), dma((2,)), dma((2,)),
         ],
         compiler_params=pltpu.CompilerParams(
             collective_id=0, has_side_effects=True, vmem_limit_bytes=24 * 1024 * 1024

time: 28.6 us -> 28.2 us (0.986)
  Pallas kernels: 27.2 us -> 26.8 us
    pallas_call x1, Pallas kernels: 26.3 us -> 26 us  [sparse_program(): pl.pallas_call(functools.partial(sparse_kernel, n_row, n_col), name='nets...]
where the time goes in v6:
time: 28.2 us; the launch traced here: 28.1 us
  Pallas kernels  26.8 us (95%)
  between operations  0.65 us (2%)
  loops' own time  0.62 us (2%)
    pallas_call x1, Pallas kernels, sparse_program(): pl.pallas_call(functools.partial(sparse_kernel, n_row, n_col), name='nets...  26 us
    pallas_call x1, Pallas kernels, sparse_program(): pl.pallas_call(finish_kernel, name='finish', out_shape=(shape((tile_r, ti...  0.84 us
    another operation x1, loops' own time, per_device(): lax.while_loop(lambda state: state[3][0, 0] > 1e+20, again, (rudy, inflat...  0.62 us

profile of v6, /device:TPU:1, one launch (start us, length us, event | category | flops | bytes accessed | tf_op | source)
XLA Modules:
  0.0 28.1 jit_solution(5949980038745791012)
XLA Ops:
  0.6 26.0 %nets_to_tiles.1 = (f32[512,128]{1,0:T(8,128)S(1)}, f32[512,128]{1,0:T(8,128)S(1)}, f32[1,2048]{1,0:T(1,128)S(1)}, f32[2,128]{1,0:T(2,128)S(1)}) custom-call(s32[4,2048]{1,0:T(4,128)} %boxes_h.1, s32[1,2048]{1,0:T(1,128)} %bitcast.83, f32[512,128]{1,0:T(8,128)} %cap_h.1, s32[1,2048]{1,0:T(1,128)} %cbin_h.1, f32[1,2048]{1,0:T(1,128)} %area_h.1), custom_call_target="tpu_custom_call" | custom-call | tf_op jit(solution)/shard_map/nets_to_tiles/pallas_call | solution.py:368
  26.6 0.8 %finish.1 = (f32[512,128]{1,0:T(8,128)}, f32[512,128]{1,0:T(8,128)}, f32[1,2048]{1,0:T(1,128)}, f32[1,128]{1,0:T(1,128)}) custom-call(f32[512,128]{1,0:T(8,128)S(1)} %get-tuple-element.216.rudy, f32[512,128]{1,0:T(8,128)S(1)} %get-tuple-element.217.infl, f32[1,2048]{1,0:T(1,128)S(1)} %get-tuple-element.218.grown, f32[2,128]{1,0:T(2,128)S(1)} %get-tuple-element.219.totals), custom_call_target="tpu_custom_call" | custom-call | tf_op jit(solution)/shard_map/finish/pallas_call | solution.py:396
  27.5 0.6 %while.36 = (f32[512,128]{1,0:T(8,128)}, f32[512,128]{1,0:T(8,128)}, f32[1,2048]{1,0:T(1,128)}, f32[1,128]{1,0:T(1,128)}, s32[4,2048]{1,0:T(4,128)}, /*index=5*/...) while((f32[512,128]{1,0:T(8,128)}, ...), condition=%wide.region_8.9_spmd, body=%wide.region_0.8_spmd.sunk | while | flops 676364864 | bytes 11909514 | solution.py:463

commit v7 on v6

--- a/solution.py
+++ b/solution.py
@@ -203,24 +203,12 @@
     bins = cbin[...]
     bin_row = (bins // tile_c).astype(F32)
     bin_col = (bins % tile_c).astype(F32)
-    for h in range(tile_r // 256):
-        onehot[h * 256 : (h + 1) * 256, :] = ones_where(
-            iota((256, cells), 0, BF16)
-            == jnp.broadcast_to((bin_row - 256.0 * h).astype(BF16), (256, cells))
-        )
-    in_col = iota((tile_c, cells), 0, BF16) == jnp.broadcast_to(bin_col.astype(BF16), (tile_c, cells))
-    area_hi, area_lo = split2(area[...])
-    nought = jnp.zeros((), BF16)
-    by_col = jnp.concatenate(
-        [
-            jnp.where(in_col, jnp.broadcast_to(area_hi, (tile_c, cells)), nought),
-            jnp.where(in_col, jnp.broadcast_to(area_lo, (tile_c, cells)), nought),
-        ],
-        axis=0,
-    )
-    bin_area = dot_nt(onehot[...], by_col)
-    bin_area = bin_area[:, :tile_c] + bin_area[:, tile_c:]
-    early_s[...] = jnp.sum(bin_area, axis=0, keepdims=True)
+    by_lane = jnp.zeros((tile_c, LANES), F32)
+    sub = iota((tile_c, LANES), 0)
+    for j in range(cells // LANES):
+        part = slice(j * LANES, (j + 1) * LANES)
+        by_lane = by_lane + jnp.where(sub == bin_col[:, part], area[:, part], 0.0)
+    early_s[...] = jnp.sum(by_lane.T, axis=0, keepdims=True)
 
     pl.semaphore_wait(barrier, chips + n_row - 1)
     swap = pltpu.make_async_remote_copy(
@@ -248,6 +236,23 @@
     spill[...] = over
 
     await_bytes(early_r, n_row - 1, early_sem.at[0])
+    for h in range(tile_r // 256):
+        onehot[h * 256 : (h + 1) * 256, :] = ones_where(
+            iota((256, cells), 0, BF16)
+            == jnp.broadcast_to((bin_row - 256.0 * h).astype(BF16), (256, cells))
+        )
+    in_col = iota((tile_c, cells), 0, BF16) == jnp.broadcast_to(bin_col.astype(BF16), (tile_c, cells))
+    area_hi, area_lo = split2(area[...])
+    nought = jnp.zeros((), BF16)
+    by_col = jnp.concatenate(
+        [
+            jnp.where(in_col, jnp.broadcast_to(area_hi, (tile_c, cells)), nought),
+            jnp.where(in_col, jnp.broadcast_to(area_lo, (tile_c, cells)), nought),
+        ],
+        axis=0,
+    )
+    bin_area = dot_nt(onehot[...], by_col)
+    bin_area = bin_area[:, :tile_c] + bin_area[:, tile_c:]
     w_hi, w_lo = split2(bin_area)
     upper = ones_where(iota((tile_r, tile_r), 0) <= iota((tile_r, tile_r), 1))
     below = dot(upper, jnp.concatenate([w_hi, w_lo], axis=1))

time: 28.2 us -> 27.8 us (0.986)
  Pallas kernels: 26.8 us -> 26.4 us
    pallas_call x1, Pallas kernels: 26 us -> 25.6 us  [sparse_program(): pl.pallas_call(functools.partial(sparse_kernel, n_row, n_col), name='nets...]
where the time goes in v7:
time: 27.8 us; the launch traced here: 27.7 us
  Pallas kernels  26.4 us (95%)
  between operations  0.65 us (2%)
  loops' own time  0.62 us (2%)
    pallas_call x1, Pallas kernels, sparse_program(): pl.pallas_call(functools.partial(sparse_kernel, n_row, n_col), name='nets...  25.6 us
    pallas_call x1, Pallas kernels, sparse_program(): pl.pallas_call(finish_kernel, name='finish', out_shape=(shape((tile_r, ti...  0.84 us
    another operation x1, loops' own time, per_device(): lax.while_loop(lambda state: state[3][0, 0] > 1e+20, again, (rudy, inflat...  0.62 us

profile of v7, /device:TPU:1, one launch (start us, length us, event | category | flops | bytes accessed | tf_op | source)
XLA Modules:
  0.0 27.7 jit_solution(15984982767319537595)
XLA Ops:
  0.6 25.6 %nets_to_tiles.1 = (f32[512,128]{1,0:T(8,128)S(1)}, f32[512,128]{1,0:T(8,128)S(1)}, f32[1,2048]{1,0:T(1,128)S(1)}, f32[2,128]{1,0:T(2,128)S(1)}) custom-call(s32[4,2048]{1,0:T(4,128)} %boxes_h.1, s32[1,2048]{1,0:T(1,128)} %bitcast.83, f32[512,128]{1,0:T(8,128)} %cap_h.1, s32[1,2048]{1,0:T(1,128)} %cbin_h.1, f32[1,2048]{1,0:T(1,128)} %area_h.1), custom_call_target="tpu_custom_call" | custom-call | tf_op jit(solution)/shard_map/nets_to_tiles/pallas_call | solution.py:373
  26.2 0.8 %finish.1 = (f32[512,128]{1,0:T(8,128)}, f32[512,128]{1,0:T(8,128)}, f32[1,2048]{1,0:T(1,128)}, f32[1,128]{1,0:T(1,128)}) custom-call(f32[512,128]{1,0:T(8,128)S(1)} %get-tuple-element.216.rudy, f32[512,128]{1,0:T(8,128)S(1)} %get-tuple-element.217.infl, f32[1,2048]{1,0:T(1,128)S(1)} %get-tuple-element.218.grown, f32[2,128]{1,0:T(2,128)S(1)} %get-tuple-element.219.totals), custom_call_target="tpu_custom_call" | custom-call | tf_op jit(solution)/shard_map/finish/pallas_call | solution.py:401
  27.0 0.6 %while.36 = (f32[512,128]{1,0:T(8,128)}, f32[512,128]{1,0:T(8,128)}, f32[1,2048]{1,0:T(1,128)}, f32[1,128]{1,0:T(1,128)}, s32[4,2048]{1,0:T(4,128)}, /*index=5*/...) while((f32[512,128]{1,0:T(8,128)}, ...), condition=%wide.region_8.9_spmd, body=%wide.region_0.8_spmd.sunk | while | flops 676364864 | bytes 11909514 | solution.py:468
